TPU v7x, 32 devices: a 4x4x1 block of a 4x4x8 slice. The times are simulated.
32 devices in a mesh: rep: 1 (over z), dp: 32 (over x, y, core).
Axes of the slice: x: 4, y: 4, z: 1, core: 2. Of those that a mesh axis runs over, the one named last changes fastest.
The devices are a block of a 4x4x8 slice.
Arguments:
- x: bfloat16 [32, 2048, 1024], P(('rep', 'dp'))
- dy: bfloat16 [32, 2048, 1024], P(('rep', 'dp'))
- w_gate: bfloat16 [2, 1024, 2816], P(None, 'dp')
- w_up: bfloat16 [2, 1024, 2816], P(None, 'dp')
- w_down: bfloat16 [2, 2816, 1024], P(None, 'dp')
- m_w_gate: float32 [2, 1024, 2816], P(None, 'dp')
- m_w_up: float32 [2, 1024, 2816], P(None, 'dp')
- m_w_down: float32 [2, 2816, 1024], P(None, 'dp')
- v_w_gate: float32 [2, 1024, 2816], P(None, 'dp')
- v_w_up: float32 [2, 1024, 2816], P(None, 'dp')
- v_w_down: float32 [2, 2816, 1024], P(None, 'dp')
Outputs:
- output 1: bfloat16 [2, 1024, 2816], P('rep', 'dp')
- output 2: bfloat16 [2, 1024, 2816], P('rep', 'dp')
- output 3: bfloat16 [2, 2816, 1024], P('rep', 'dp')
- output 4: float32 [2, 1024, 2816], P('rep', 'dp')
- output 5: float32 [2, 1024, 2816], P('rep', 'dp')
- output 6: float32 [2, 2816, 1024], P('rep', 'dp')
- output 7: float32 [2, 1024, 2816], P('rep', 'dp')
- output 8: float32 [2, 1024, 2816], P('rep', 'dp')
- output 9: float32 [2, 2816, 1024], P('rep', 'dp')
All inputs are finite; a program needn't handle non-finite values.
Results may differ from a plain program's by a relative error of at most 0.022.
Values are sent between devices in bfloat16 or wider.
A program may use at most 768 MiB of HBM per device.

v0:
```python
import jax
import jax.numpy as jnp
from jax import lax
from jax.sharding import PartitionSpec as P

NAMES = ("w_gate", "w_up", "w_down")


def matmul(a, w):
    return jnp.dot(a, w, preferred_element_type=jnp.float32).astype(jnp.bfloat16)


def normed(h):
    wide = h.astype(jnp.float32)
    scale = lax.rsqrt(jnp.mean(wide**2, -1, keepdims=True) + 1e-6)
    return (wide * scale).astype(jnp.bfloat16)


def layer(h, w):
    a = normed(h)
    gate = jnp.dot(a, w["w_gate"], preferred_element_type=jnp.float32)
    up = jnp.dot(a, w["w_up"], preferred_element_type=jnp.float32)
    return h + matmul((jax.nn.silu(gate) * up).astype(jnp.bfloat16), w["w_down"])


def adamw(w, m, v, g):
    m = 0.9 * m + 0.1 * g
    v = 0.95 * v + 0.05 * g * g
    step = m * lax.rsqrt(v + 1e-8) + 0.1 * w
    return (w - 0.02 * step).astype(jnp.bfloat16), m, v


def clipped(gradients, sum_of_squares, count):
    factor = jnp.minimum(1.0, 0.5 * lax.rsqrt(sum_of_squares / count + 1e-30))
    return [g * factor for g in gradients]


def solution(mesh):
    def fetched(weights, number):
        return {name: lax.all_gather(w[number], "dp", axis=0, tiled=True) for name, w in zip(NAMES, weights, strict=True)}

    def step(x, dy, *arrays):
        weights, m, v = (arrays[i : i + 3] for i in (0, 3, 6))
        layers = weights[0].shape[0]
        h, kept = x[0], []
        for number in range(layers):
            kept.append(h)
            h = layer(h, fetched(weights, number))
        by_h, mine = dy[0], [None] * layers
        for number in reversed(range(layers)):
            _, back = jax.vjp(lambda w, h: layer(h, w), fetched(weights, number), kept[number])
            by_w, by_h = back(by_h)
            mine[number] = [lax.psum_scatter(by_w[name], "dp", scatter_dimension=0, tiled=True) for name in NAMES]
        gradients = [jnp.stack([mine[number][i] for number in range(layers)]).astype(jnp.float32) for i in range(3)]
        squares = lax.psum(sum(jnp.sum(g * g) for g in gradients), "dp")
        gradients = clipped(gradients, squares, lax.psum(1, "dp") * sum(g.size for g in gradients))
        new = [adamw(w.astype(jnp.float32), m, v, g) for w, m, v, g in zip(weights, m, v, gradients, strict=True)]
        return tuple(one[which] for which in range(3) for one in new)

    states, cut = P(("rep", "dp"), None, None), P(None, "dp", None)
    return jax.shard_map(
        step,
        mesh=mesh,
        in_specs=(states, states) + (cut,) * 9,
        out_specs=(P("rep", "dp", None),) * 9,
        check_vma=False,
    )
```

profile of v0, /device:TPU:97, one launch (start us, length us, event | category | flops | bytes accessed | tf_op | source)
XLA Modules:
  0.0 920.5 jit_solution(11674824794985975622)
XLA Ops:
  31.0 26.9 %all-gather.13.cloned.1.call-done = bf16[1,1024,2816]{2,1,0:T(8,128)(2,1)} async-done(((bf16[1,32,2816]{2,1,0:T(8,128)(2,1)}), bf16[1,1024,2816]{2,1,0:T(8,128)(2,1)}) %all-gather.13.cloned.1.call-update) | async-done | bytes 5767184 | tf_op jit(solution)/shard_map/all_gather | solution.py:40
  57.9 20.0 %fusion.35 = f32[2048,2816]{1,0:T(8,128)} fusion(bf16[1,1024,2816]{2,1,0:T(8,128)(2,1)} %all-gather.13.cloned.1.call-done, bf16[1,2048,1024]{1,2,0:T(8,128)(2,1)} %copy.20, f32[2048]{0:T(1024)S(1)} %add_rsqrt_fusion), kind=kOutput, calls=%fused_computation.53 | convolution fusion | flops 11817451520 | bytes 33038336 | tf_op jit(solution)/shard_map/dot_general | solution.py:21
  77.9 24.5 %all-gather.15.cloned.1.call-done = bf16[1,1024,2816]{2,1,0:T(8,128)(2,1)} async-done(((bf16[1,32,2816]{2,1,0:T(8,128)(2,1)}), bf16[1,1024,2816]{2,1,0:T(8,128)(2,1)}) %all-gather.15.cloned.1.call-update) | async-done | bytes 5767184 | tf_op jit(solution)/shard_map/all_gather | solution.py:40
  102.4 27.8 %multiply_convert_fusion.1 = (bf16[2048,2816]{1,0:T(8,128)(2,1)}, f32[2048,2816]{1,0:T(8,128)}) fusion(f32[2048,2816]{1,0:T(8,128)} %fusion.35, bf16[1,1024,2816]{2,1,0:T(8,128)(2,1)} %all-gather.15.cloned.1.call-done, bf16[1,2048,1024]{1,2,0:T(8,128)(2,1)} %copy.20, f32[2048]{0:T(1024)S(1)} %add_rsqrt_fusion), kind=kOutput, calls=%fused_computation.17 | convolution fusion | flops 11852054528 | bytes 67641344 | tf_op jit(solution)/shard_map/dot_general | solution.py:22
  146.9 19.8 %fusion.19 = (f32[2048]{0:T(1024)S(1)}, bf16[2048,1024]{0,1:T(8,128)(2,1)}) fusion(bf16[2048,2816]{1,0:T(8,128)(2,1)} %get-tuple-element.24, bf16[1,2816,1024]{2,1,0:T(8,128)(2,1)} %all-gather.17.cloned.1.call-done, bf16[1,2048,1024]{1,2,0:T(8,128)(2,1)} %copy.20), kind=kOutput, calls=%fused_computation.37 | convolution fusion | flops 11821643776 | bytes 25698304 | tf_op jit(solution)/shard_map/dot_general | solution.py:10
  166.7 24.5 %all-gather.21.cloned.1.call-done = bf16[1,2816,1024]{2,1,0:T(8,128)(2,1)} async-done(((bf16[1,88,1024]{2,1,0:T(8,128)(2,1)}), bf16[1,2816,1024]{2,1,0:T(8,128)(2,1)}) %all-gather.21.cloned.1.call-update) | async-done | bytes 5767184 | tf_op jit(solution)/shard_map/all_gather | solution.py:40
  209.4 26.2 %all-gather.23.cloned.1.call-done = bf16[1,1024,2816]{2,1,0:T(8,128)(2,1)} async-done(((bf16[1,32,2816]{2,1,0:T(8,128)(2,1)}), bf16[1,1024,2816]{2,1,0:T(8,128)(2,1)}) %all-gather.23.cloned.1.call-update) | async-done | bytes 5767184 | tf_op jit(solution)/shard_map/all_gather | solution.py:40
  235.6 20.1 %fusion.22 = f32[2048,2816]{1,0:T(8,128)} fusion(bf16[1,1024,2816]{2,1,0:T(8,128)(2,1)} %all-gather.23.cloned.1.call-done, bf16[2048,1024]{0,1:T(8,128)(2,1)} %get-tuple-element.27, f32[2048]{0:T(1024)S(1)} %fusion.80), kind=kOutput, calls=%fused_computation.40 | convolution fusion | flops 11817451520 | bytes 33038336 | tf_op jit(solution)/shard_map/jvp()/dot_general | solution.py:22
  255.6 24.3 %all-gather.19.cloned.1.call-done = bf16[1,1024,2816]{2,1,0:T(8,128)(2,1)} async-done(((bf16[1,32,2816]{2,1,0:T(8,128)(2,1)}), bf16[1,1024,2816]{2,1,0:T(8,128)(2,1)}) %all-gather.19.cloned.1.call-update) | async-done | bytes 5767184 | tf_op jit(solution)/shard_map/all_gather | solution.py:40
  279.9 34.4 %fusion.2 = (bf16[2048,2816]{1,0:T(8,128)(2,1)}, f32[2048,2816]{1,0:T(8,128)}) fusion(f32[2048,2816]{1,0:T(8,128)} %fusion.22, bf16[2048,2816]{1,0:T(8,128)(2,1)} %convolution_convert_fusion.1, bf16[1,1024,2816]{2,1,0:T(8,128)(2,1)} %all-gather.19.cloned.1.call-done, bf16[2048,1024]{0,1:T(8,128)(2,1)} %get-tuple-element.27, f32[2048]{0:T(1024)S(1)} %fusion.80), kind=kOutput, calls=%fused_computation.8 | convolution fusion | flops 11886657536 | bytes 79175680 | tf_op jit(solution)/shard_map/jvp()/dot_general | solution.py:21
  314.3 21.7 %fusion.12 = bf16[2048,1024]{0,1:T(8,128)(2,1)} fusion(bf16[2048,2816]{1,0:T(8,128)(2,1)} %convolution_convert_fusion.1, bf16[1,1024,2816]{2,1,0:T(8,128)(2,1)} %all-gather.23.cloned.1.call-done, f32[2048,2816]{1,0:T(8,128)} %get-tuple-element.29), kind=kOutput, calls=%fused_computation.21 | convolution fusion | flops 11845763072 | bytes 44564480 | tf_op jit(solution)/shard_map/transpose(jvp())/dot_general | solution.py:22
  336.0 18.9 %fusion.21 = (f32[2048]{0:T(1024)S(1)}, bf16[2048,1024]{0,1:T(8,128)(2,1)S(1)}) fusion(bf16[2048,1024]{0,1:T(8,128)(2,1)} %get-tuple-element.27, bf16[2048,1024]{0,1:T(8,128)(2,1)} %fusion.12, bf16[2048,2816]{1,0:T(8,128)(2,1)} %get-tuple-element.28, bf16[1,1024,2816]{2,1,0:T(8,128)(2,1)} %all-gather.19.cloned.1.call-done), kind=kOutput, calls=%fused_computation.39 | convolution fusion | flops 11821643776 | bytes 29892608 | tf_op jit(solution)/shard_map/transpose(jvp())/dot_general | solution.py:21
  377.8 23.6 %fusion.37 = bf16[2816,1024]{1,0:T(8,128)(2,1)} fusion(f32[2048,2816]{1,0:T(8,128)} %fusion.22, bf16[1,2048,1024]{2,1,0:T(8,128)(2,1)} %param.12, f32[2048,2816]{1,0:T(8,128)} %get-tuple-element.29), kind=kOutput, calls=%fused_computation.55 | convolution fusion | flops 11848646656 | bytes 56098816 | tf_op jit(solution)/shard_map/transpose(jvp())/dot_general | solution.py:10
  401.5 18.5 %convolution_convert_fusion = bf16[2048,2816]{1,0:T(8,128)(2,1)} fusion(bf16[2048,1024]{0,1:T(8,128)(2,1)} %copy-done.2, bf16[1,2816,1024]{2,1,0:T(8,128)(2,1)} %all-gather.17.cloned.1.call-done), kind=kOutput, calls=%fused_computation.28 | convolution fusion | flops 11816927232 | bytes 21495808 | tf_op jit(solution)/shard_map/transpose(jvp())/dot_general | solution.py:10
  420.0 22.5 %fusion.42 = bf16[1024,2816]{1,0:T(8,128)(2,1)} fusion(bf16[2048,2816]{1,0:T(8,128)(2,1)} %convolution_convert_fusion, f32[2048,2816]{1,0:T(8,128)} %fusion.35, bf16[1,2048,1024]{1,2,0:T(8,128)(2,1)} %copy.20, f32[2048]{0:T(1024)S(1)} %copy-done.14), kind=kOutput, calls=%fused_computation.58 | convolution fusion | flops 11854938112 | bytes 44572672 | tf_op jit(solution)/shard_map/transpose(jvp())/dot_general | solution.py:22
  442.7 22.7 %fusion.38 = bf16[1024,2816]{1,0:T(8,128)(2,1)} fusion(bf16[2048,2816]{1,0:T(8,128)(2,1)} %convolution_convert_fusion.1, bf16[2048,1024]{0,1:T(8,128)(2,1)} %get-tuple-element.27, f32[2048]{0:T(1024)S(1)} %copy-done.10, f32[2048,2816]{1,0:T(8,128)} %get-tuple-element.29), kind=kOutput, calls=%fused_computation.56 | convolution fusion | flops 11854938112 | bytes 44572672 | tf_op jit(solution)/shard_map/transpose(jvp())/dot_general | solution.py:22
  465.6 27.0 %fusion.39 = bf16[1024,2816]{1,0:T(8,128)(2,1)} fusion(f32[2048,2816]{1,0:T(8,128)} %fusion.35, f32[2048,2816]{1,0:T(8,128)} %get-tuple-element.25, bf16[2048,2816]{1,0:T(8,128)(2,1)} %convolution_convert_fusion, bf16[1,2048,1024]{1,2,0:T(8,128)(2,1)} %copy.20, f32[2048]{0:T(1024)S(1)} %copy-done.14), kind=kOutput, calls=%fused_computation.57 | convolution fusion | flops 11883773952 | bytes 67641344 | tf_op jit(solution)/shard_map/transpose(jvp())/dot_general | solution.py:21
  492.7 19.0 %convolution_convert_fusion.3 = bf16[1024,2816]{1,0:T(8,128)(2,1)} fusion(bf16[2048,2816]{1,0:T(8,128)(2,1)} %get-tuple-element.28, bf16[2048,1024]{0,1:T(8,128)(2,1)} %get-tuple-element.27, f32[2048]{0:T(1024)S(1)} %copy-done.10), kind=kOutput, calls=%fused_computation.60 | convolution fusion | flops 11817451520 | bytes 21504000 | tf_op jit(solution)/shard_map/transpose(jvp())/dot_general | solution.py:21
  511.9 21.4 %reduce-scatter.17.cloned.1.call-done = bf16[88,1024]{1,0:T(8,128)(2,1)} async-done(((bf16[2816,1024]{1,0:T(8,128)(2,1)}), bf16[88,1024]{1,0:T(8,128)(2,1)}) %reduce-scatter.17.cloned.1.call-update) | async-done | bytes 180240 | tf_op jit(solution)/shard_map/reduce_scatter | solution.py:53
  535.0 79.0 %reduce-scatter.11.cloned.1.call-done = bf16[32,2816]{1,0:T(8,128)(2,1)} async-done(((bf16[1024,2816]{1,0:T(8,128)(2,1)}), bf16[32,2816]{1,0:T(8,128)(2,1)}) %reduce-scatter.11.cloned.1.call-update) | async-done | bytes 180240 | tf_op jit(solution)/shard_map/reduce_scatter | solution.py:53
  614.0 80.7 %reduce-scatter.13.cloned.1.call-done = bf16[32,2816]{1,0:T(8,128)(2,1)} async-done(((bf16[1024,2816]{1,0:T(8,128)(2,1)}), bf16[32,2816]{1,0:T(8,128)(2,1)}) %reduce-scatter.13.cloned.1.call-update) | async-done | bytes 180240 | tf_op jit(solution)/shard_map/reduce_scatter | solution.py:53
  696.5 79.0 %reduce-scatter.7.cloned.1.call-done = bf16[32,2816]{1,0:T(8,128)(2,1)} async-done(((bf16[1024,2816]{1,0:T(8,128)(2,1)}), bf16[32,2816]{1,0:T(8,128)(2,1)}) %reduce-scatter.7.cloned.1.call-update) | async-done | bytes 180240 | tf_op jit(solution)/shard_map/reduce_scatter | solution.py:53
  775.4 80.6 %reduce-scatter.9.cloned.1.call-done = bf16[32,2816]{1,0:T(8,128)(2,1)} async-done(((bf16[1024,2816]{1,0:T(8,128)(2,1)}), bf16[32,2816]{1,0:T(8,128)(2,1)}) %reduce-scatter.9.cloned.1.call-update) | async-done | bytes 180240 | tf_op jit(solution)/shard_map/reduce_scatter | solution.py:53
  859.7 46.3 %psum.7 = f32[]{:T(128)} all-reduce(f32[]{:T(128)S(6)} %add.99), channel_id=1, replica_groups=mesh['rep'=1,'dp'=32] {'dp'}, use_global_device_ids=true, to_apply=%region_12.13 | all-reduce | flops 1 | bytes 8 | tf_op jit(solution)/shard_map/psum | solution.py:55
  (73 shorter events, 93.9 us)
Async XLA Ops:
  7.2 50.7 %all-gather.13.cloned.1.call-start = ((), (), s32[]{:S(2)}) async-start(), calls=%async_computation.12 | async-start | bytes 5947392 | tf_op jit(solution)/shard_map/all_gather | solution.py:40
  9.1 93.3 %all-gather.15.cloned.1.call-start = ((), (), s32[]{:S(2)}) async-start(), calls=%async_computation.13 | async-start | bytes 5947392 | tf_op jit(solution)/shard_map/all_gather | solution.py:40
  11.0 135.9 %all-gather.17.cloned.1.call-start = ((), (), s32[]{:S(2)}) async-start(), calls=%async_computation.14 | async-start | bytes 5947392 | tf_op jit(solution)/shard_map/all_gather | solution.py:40
  12.9 178.3 %all-gather.21.cloned.1.call-start = ((), (), s32[]{:S(2)}) async-start(), calls=%async_computation.16 | async-start | bytes 5947392 | tf_op jit(solution)/shard_map/all_gather | solution.py:40
  13.5 222.0 %all-gather.23.cloned.1.call-start = ((), (), s32[]{:S(2)}) async-start(), calls=%async_computation.17 | async-start | bytes 5947392 | tf_op jit(solution)/shard_map/all_gather | solution.py:40
  14.2 265.7 %all-gather.19.cloned.1.call-start = ((), (), s32[]{:S(2)}) async-start(), calls=%async_computation.15 | async-start | bytes 5947392 | tf_op jit(solution)/shard_map/all_gather | solution.py:40
  14.8 497.0 %reduce-scatter.15.cloned.1.call-start = ((), (), s32[]{:S(2)}) async-start(), calls=%async_computation.10 | async-start | bytes 5947392 | tf_op jit(solution)/shard_map/reduce_scatter | solution.py:53
  24.5 77.9 %copy-start.13 = (f32[2048]{0:T(1024)}, f32[2048]{0:T(1024)S(1)}, u32[]{:S(2)}) copy-start(f32[2048]{0:T(1024)S(1)} %add_rsqrt_fusion) | copy-start | bytes 24580
  166.7 42.7 %copy-start.11 = (f32[2048]{0:T(1024)}, f32[2048]{0:T(1024)S(1)}, u32[]{:S(2)}) copy-start(f32[2048]{0:T(1024)S(1)} %get-tuple-element.26) | copy-start | bytes 24580
  166.7 188.2 %copy-start.9 = (f32[2048]{0:T(1024)}, f32[2048]{0:T(1024)S(1)}, u32[]{:S(2)}) copy-start(f32[2048]{0:T(1024)S(1)} %fusion.80) | copy-start | bytes 24580
  335.9 18.9 %copy-start = (bf16[1,2048,1024]{1,2,0:T(8,128)(2,1)S(1)}, bf16[1,2048,1024]{1,2,0:T(8,128)(2,1)}, u32[]{:S(2)}) copy-start(bf16[1,2048,1024]{1,2,0:T(8,128)(2,1)} %copy.21) | copy-start | bytes 12582916
  335.9 18.9 %copy-start.1 = (bf16[2048,1024]{0,1:T(8,128)(2,1)S(1)}, bf16[2048,1024]{0,1:T(8,128)(2,1)}, u32[]{:S(2)}) copy-start(bf16[2048,1024]{0,1:T(8,128)(2,1)} %get-tuple-element.27) | copy-start | bytes 12582916
  377.7 155.5 %reduce-scatter.17.cloned.1.call-start = ((), (), s32[]{:S(2)}) async-start(), calls=%async_computation.11 | async-start | bytes 5947392 | tf_op jit(solution)/shard_map/reduce_scatter | solution.py:53
  401.4 212.5 %reduce-scatter.11.cloned.1.call-start = ((), (), s32[]{:S(2)}) async-start(), calls=%async_computation.8 | async-start | bytes 5947392 | tf_op jit(solution)/shard_map/reduce_scatter | solution.py:53
  420.0 22.7 %copy-start.10 = (f32[2048]{0:T(1024)S(1)}, f32[2048]{0:T(1024)}, u32[]{:S(2)}) copy-start(f32[2048]{0:T(1024)} %copy-done.9) | copy-start | bytes 24580
  442.6 252.0 %reduce-scatter.13.cloned.1.call-start = ((), (), s32[]{:S(2)}) async-start(), calls=%async_computation.9 | async-start | bytes 5947392 | tf_op jit(solution)/shard_map/reduce_scatter | solution.py:53
  465.5 309.9 %reduce-scatter.7.cloned.1.call-start = ((), (), s32[]{:S(2)}) async-start(), calls=%async_computation.6 | async-start | bytes 5947392 | tf_op jit(solution)/shard_map/reduce_scatter | solution.py:53
  492.6 414.1 %copy-start.5 = (bf16[2,88,1024]{2,1,0:T(8,128)(2,1)S(1)}, bf16[2,88,1024]{2,1,0:T(8,128)(2,1)}, u32[]{:S(2)}) copy-start(bf16[2,88,1024]{2,1,0:T(8,128)(2,1)} %param.15) | copy-start | bytes 1081348
  492.6 414.1 %copy-start.6 = (f32[2,88,1024]{2,1,0:T(8,128)S(1)}, f32[2,88,1024]{2,1,0:T(8,128)}, u32[]{:S(2)}) copy-start(f32[2,88,1024]{2,1,0:T(8,128)} %param.21) | copy-start | bytes 2162692
  492.7 414.1 %copy-start.7 = (f32[2,88,1024]{2,1,0:T(8,128)S(1)}, f32[2,88,1024]{2,1,0:T(8,128)}, u32[]{:S(2)}) copy-start(f32[2,88,1024]{2,1,0:T(8,128)} %param.18) | copy-start | bytes 2162692
  492.7 363.3 %reduce-scatter.9.cloned.1.call-start = ((), (), s32[]{:S(2)}) async-start(), calls=%async_computation.7 | async-start | bytes 5947392 | tf_op jit(solution)/shard_map/reduce_scatter | solution.py:53
  511.8 397.4 %copy-start.3 = (bf16[2,32,2816]{2,1,0:T(8,128)(2,1)S(1)}, bf16[2,32,2816]{2,1,0:T(8,128)(2,1)}, u32[]{:S(2)}) copy-start(bf16[2,32,2816]{2,1,0:T(8,128)(2,1)} %param.13) | copy-start | bytes 1081348
  511.8 397.4 %copy-start.4 = (bf16[2,32,2816]{2,1,0:T(8,128)(2,1)S(1)}, bf16[2,32,2816]{2,1,0:T(8,128)(2,1)}, u32[]{:S(2)}) copy-start(bf16[2,32,2816]{2,1,0:T(8,128)(2,1)} %param.14) | copy-start | bytes 1081348
  511.8 397.4 %copy-start.8 = (f32[2,32,2816]{2,1,0:T(8,128)S(1)}, f32[2,32,2816]{2,1,0:T(8,128)}, u32[]{:S(2)}) copy-start(f32[2,32,2816]{2,1,0:T(8,128)} %param.19) | copy-start | bytes 2162692
  (3 other events, 39.5 us)
Sparse Core Ops, SparseCore 0:
  10.7 47.2 all-gather.12
  60.6 41.7 all-gather.14
  105.1 41.7 all-gather.16
  149.4 41.7 all-gather.20
  193.7 41.7 all-gather.22
  238.1 41.7 all-gather.18
  377.8 74.5 reduce-scatter.14
  456.0 77.1 reduce-scatter.16
  536.8 77.1 reduce-scatter.10
  617.4 77.1 reduce-scatter.12
  698.2 77.1 reduce-scatter.6
  778.8 77.1 reduce-scatter.8
where the time goes:
time: 930 us; the launch traced here: 920 us
  waiting for transfers between devices  486 us (52%)
  matrix products  331 us (36%)
  blocking collectives  46.3 us (5%)
  local copies, waits for them, and re-layouts  20.4 us (2%)
  other arithmetic  18.5 us (2%)
  between operations  17.5 us (2%)
    reduce_scatter x6, waiting for transfers between devices, step(): lax.psum_scatter(by_w[name], 'dp', scatter_dimension=0, tiled=True)  341 us
    all_gather x6, waiting for transfers between devices, fetched(): lax.all_gather(w[number], 'dp', axis=0, tiled=True)  143 us
    dot_general x5, matrix products, layer(): gate = jnp.dot(a, w['w_gate'], preferred_element_type=jnp.float32)  119 us
    dot_general x5, matrix products, layer(): up = jnp.dot(a, w['w_up'], preferred_element_type=jnp.float32)  115 us
    dot_general x5, matrix products, matmul(): jnp.dot(a, w, preferred_element_type=jnp.float32).astype(jnp.bfloat16)  97.2 us
    psum x1, blocking collectives, step(): squares = lax.psum(sum((jnp.sum(g * g) for g in gradients)), 'dp')  46.3 us
  transfers between devices with their start and end apart: 12, of which 11 were waited for; matrix products, arithmetic and copies ran while one was open for 29% of the time, Pallas kernels for 0%

commit v1 on v0

v1 whole, which is shorter than its diff:
```python
import functools, math
import jax, jax.numpy as jnp
from jax import lax
from jax.experimental import pallas as pl
from jax.experimental.pallas import tpu as pltpu
from jax.sharding import PartitionSpec as P
MESH = pl.DeviceIdType.MESH
bf = jnp.bfloat16

class Place:
    def __init__(self, n):
        self.side = side = math.isqrt(n // 2)
        me = lax.axis_index("dp")
        self.c = c = lax.rem(me, 2)
        chip = me // 2
        x, y = chip // side, lax.rem(chip, side)
        self.i1 = x + c * (y - x)
        self.i2 = y + c * (x - y)
        self.m1 = side + c * (1 - side)
        self.m2 = 1 + c * (side - 1)
        self.partner = me + 1 - 2 * c
    def mod(self, a):
        return lax.rem(a + 2 * self.side, self.side)
    def chip(self, j1, j2):
        return j1 * self.m1 + j2 * self.m2
    def next1(self, d):
        return 2 * self.chip(self.mod(self.i1 + d), self.i2) + self.c
    def next2(self, d):
        return 2 * self.chip(self.i1, self.mod(self.i2 + d)) + self.c

def barrier(p):
    sem = pltpu.get_barrier_semaphore()
    others = [p.partner, p.next1(1), p.next1(-1), p.next2(1), p.next2(-1)]
    for o in others:
        pl.semaphore_signal(sem, inc=1, device_id={"dp": o}, device_id_type=MESH)
    pl.semaphore_wait(sem, len(others))

DIRS = (1, -1)

class Gather:
    STAGES = 8
    def __init__(self, p, own, block, group, sems):
        self.p, self.own, self.block, self.group = p, own, block, group
        self.local, self.s1, self.r1, self.s2, self.r2, self.sd, self.rd = sems
    def remote(self, src, dst, s, r, dev):
        return pltpu.make_async_remote_copy(src_ref=src, dst_ref=dst, send_sem=s, recv_sem=r, device_id={"dp": dev}, device_id_type=MESH)
    def c1(self, j, e, k):
        p, d = self.p, DIRS[e]
        here = self.block(j, e, p.mod(p.i1 - d * k), p.i2)
        return self.remote(self.own(j, e) if k == 0 else here, here, self.s1.at[j, e, k], self.r1.at[j, e, k], p.next1(d))
    def c2(self, j, e, k, core):
        p, d = self.p, DIRS[e]
        g = self.group(j, e, core, p.mod(p.i2 - d * k))
        return self.remote(g, g, self.s2.at[j, e, k], self.r2.at[j, e, k], p.next2(d))
    def cd(self, j, e, k, core):
        p, d = self.p, DIRS[e]
        g = self.group(j, e, core, p.mod(p.i2 - d * k))
        return self.remote(g, g, self.sd.at[j, e, k], self.rd.at[j, e, k], p.partner)
    def cl(self, j, e):
        p = self.p
        return pltpu.make_async_copy(self.own(j, e), self.block(j, e, p.i1, p.i2), self.local.at[j, e])
    def stage(self, k, j):
        p = self.p
        n = p.side
        if k == 0:
            for e in (0, 1):
                self.c1(j, e, 0).start()
                self.cl(j, e).start()
        elif k < n:
            for e in (0, 1):
                self.c1(j, e, k - 1).wait_recv()
                if k < n - 1:
                    self.c1(j, e, k).start()
            if k == n - 1:
                for e in (0, 1):
                    self.cl(j, e).wait()
                self.both(j, 0)
        elif k < 2 * n - 1:
            for e in (0, 1):
                self.c2(j, e, k - n, 0).wait_recv()
            self.both(j, k - n + 1)
        else:
            for e in (0, 1):
                for s in range(n):
                    self.cd(j, e, s, 0).wait_recv()
                    self.cd(j, e, s, 0).wait_send()
                for s in range(n - 1):
                    self.c1(j, e, s).wait_send()
                    self.c2(j, e, s, 0).wait_send()
    def both(self, j, k):
        for core in (0, 1):
            @pl.when(self.p.c == core)
            def _():
                for e in (0, 1):
                    if k < self.p.side - 1:
                        self.c2(j, e, k, core).start()
                    self.cd(j, e, k, core).start()

def gather_sems(n, side):
    D = pltpu.SemaphoreType.DMA
    return [D((n, 2)), D((n, 2, side - 1)), D((n, 2, side - 1)), D((n, 2, side - 1)), D((n, 2, side - 1)), D((n, 2, side)), D((n, 2, side))]

def gather_all(n, wg, wu, wd, lag=1, cg=256, cd=128, cid=1, order="gdg"):
    side = math.isqrt(n // 2)
    L, R, F = wg.shape
    Rd, Dm = wd.shape[1:]
    ng, nd = F // cg, Dm // (2 * cd)
    def kernel(wg_ref, wu_ref, wd_ref, og, ou, od, *sems):
        p = Place(n)
        barrier(p)
        def streams():
            out = []
            for l in range(L):
                def own(j, e, l=l):
                    return (wg_ref, wu_ref)[e].at[l, :, pl.ds(pl.multiple_of(j * cg, cg), cg)]
                def view(j, e, l=l):
                    return (og, ou)[e].at[l, :, :, :, :, pl.ds(pl.multiple_of(j * cg, cg), cg)]
                def own_d(j, e, l=l):
                    return wd_ref.at[l, :, pl.ds(pl.multiple_of((2 * j + e) * cd, cd), cd)]
                def view_d(j, e, l=l):
                    return od.at[l, :, :, :, :, pl.ds(pl.multiple_of((2 * j + e) * cd, cd), cd)]
                for own_, view_, m, s in ((own, view, ng, sems[14 * l:14 * l + 7]), (own_d, view_d, nd, sems[14 * l + 7:14 * l + 14])):
                    def block(j, e, j1, j2, view_=view_):
                        return view_(j, e).at[j1 + p.c * (j2 - j1), j2 + p.c * (j1 - j2), p.c]
                    def group(j, e, core, j2, view_=view_):
                        return view_(j, e).at[:, j2, 0] if core == 0 else view_(j, e).at[j2, :, 1]
                    out.append((Gather(p, own_, block, group, s), m))
            return out
        st = streams()
        if order == "gdg":
            st = [st[0], st[1], st[3], st[2]]
        starts, at = [], 0
        for g, m in st:
            starts.append(at); at += m
        total = at + (Gather.STAGES - 1) * lag
        def body(i, _):
            for k in reversed(range(Gather.STAGES)):
                for (g, m), lo in zip(st, starts):
                    j = i - lo - k * lag
                    @pl.when((j >= 0) & (j < m))
                    def _():
                        g.stage(k, j)
            return 0
        lax.fori_loop(0, total, body, 0)
    S = jax.ShapeDtypeStruct
    sems = []
    for l in range(L):
        sems += gather_sems(ng, side) + gather_sems(nd, side)
    V, A = pl.BlockSpec(memory_space=pltpu.VMEM), pl.BlockSpec(memory_space=pl.ANY)
    og, ou, od = pl.pallas_call(
        kernel, name="gather",
        out_shape=[S((L, side, side, 2, R, F), bf), S((L, side, side, 2, R, F), bf), S((L, side, side, 2, Rd, Dm), bf)],
        in_specs=[V] * 3, out_specs=[A] * 3, scratch_shapes=sems,
        compiler_params=pltpu.CompilerParams(collective_id=cid, has_side_effects=True, vmem_limit_bytes=48 * 2**20),
    )(wg, wu, wd)
    return og.reshape(L, n * R, F), ou.reshape(L, n * R, F), od.reshape(L, n * Rd, Dm)


f32 = jnp.float32

class Scatter:
    STAGES = 8
    def __init__(self, p, m, lag, bufs, done):
        self.p, self.m, self.lag, self.done = p, m, lag, done
        (self.own, self.q, self.snd1, self.rcv1, self.mid, self.snd2, self.rcv2,
         self.sd, self.rd, self.s1, self.r1, self.s2, self.r2) = bufs
        self.keep, self.pool = scatter_slots(m, lag)
    @staticmethod
    def remote(src, dst, s, r, dev):
        return pltpu.make_async_remote_copy(src_ref=src, dst_ref=dst, send_sem=s, recv_sem=r, device_id={"dp": dev}, device_id_type=MESH)
    def slot(self, j, h):
        mine, other = lax.rem(j, self.keep), self.keep + lax.rem(j, self.pool)
        return mine + (other - mine) * (self.p.c + h - 2 * self.p.c * h)
    def cd(self, j):
        return self.remote(self.own.at[self.keep + lax.rem(j, self.pool)], self.q.at[j], self.sd.at[j], self.rd.at[j], self.p.partner)
    def c1(self, j, e, k):
        return self.remote(self.snd1.at[lax.rem(j, self.snd1.shape[0]), e, k], self.rcv1.at[j, e, k], self.s1.at[j, e, k], self.r1.at[j, e, k], self.p.next1(DIRS[e]))
    def c2(self, j, e, k):
        return self.remote(self.snd2.at[lax.rem(j, self.snd2.shape[0]), e, k], self.rcv2.at[j, e, k], self.s2.at[j, e, k], self.r2.at[j, e, k], self.p.next2(DIRS[e]))
    def send(self, j):
        self.cd(j).start()
    def mine(self, j, e, j1, b):
        at = self.p.chip(j1, b)
        return self.own[lax.rem(j, self.keep), e, at].astype(f32) + self.q[j, e, at].astype(f32)
    def stage(self, k, j):
        p, n = self.p, self.p.side
        if k == 1:
            self.cd(j).wait_recv()
            self.cd(j).wait_send()
        elif k <= n:
            for e in (0, 1):
                self.c1(j, e, k - 2).wait_recv()
                self.c1(j, e, k - 2).wait_send()
        else:
            for e in (0, 1):
                self.c2(j, e, k - n - 1).wait_recv()
                self.c2(j, e, k - n - 1).wait_send()
        for e in (0, 1):
            d = DIRS[e]
            if k <= n:
                g = p.mod(p.i1 - d * k)
                for b in range(n):
                    v = self.mine(j, e, g, b)
                    if k > 1:
                        v = self.rcv1[j, e, k - 2, b].astype(f32) + v
                    if k < n:
                        self.snd1[lax.rem(j, self.snd1.shape[0]), e, k - 1, b] = v.astype(bf)
                    else:
                        self.mid[lax.rem(j, self.mid.shape[0]), e, b] = v
            if k >= n:
                v = self.mid[lax.rem(j, self.mid.shape[0]), e, p.mod(p.i2 - d * (k - n + 1))]
                if k > n:
                    v = self.rcv2[j, e, k - n - 1].astype(f32) + v
                if k < 2 * n - 1:
                    self.snd2[lax.rem(j, self.snd2.shape[0]), e, k - n] = v.astype(bf)
                else:
                    self.done(j, e, v)
        for e in (0, 1):
            if k < n:
                self.c1(j, e, k - 1).start()
            elif k < 2 * n - 1:
                self.c2(j, e, k - n).start()

def scatter_slots(m, lag):
    return min(m, 4 * lag), min(m, lag + 1)

def scatter_bufs(m, lag, side, R, C):
    keep, pool = scatter_slots(m, lag)
    few, V, D = min(m, lag + 1), pltpu.VMEM, pltpu.SemaphoreType.DMA
    return [V((keep + pool, 2, side * side, R, C), bf), V((m, 2, side * side, R, C), bf),
            V((few, 2, side - 1, side, R, C), bf), V((m, 2, side - 1, side, R, C), bf),
            V((min(m, 3 * lag + 1), 2, side, R, C), f32),
            V((few, 2, side - 1, R, C), bf), V((m, 2, side - 1, R, C), bf),
            D((m,)), D((m,)), D((m, 2, side - 1)), D((m, 2, side - 1)), D((m, 2, side - 1)), D((m, 2, side - 1))]

TN = (((0,), (0,)), ((), ()))

def grads(n, a, act, dgate, dup, dy, lag=2, lagd=1, cg=256, cd=128, cid=2):
    side = math.isqrt(n // 2)
    T, Dm = a.shape
    F = act.shape[1]
    R, Rd, ng, nd = Dm // n, F // n, F // cg, Dm // (2 * cd)
    half = F // 2
    chips = side * side
    def kernel(a_h, act_h, dg_h, du_h, dy_h, og, ou, od, a_v, act_v, dg_v, dy_v, ld, ldg, ldy, *bufs):
        p = Place(n)
        def load_act(m):
            cols = pl.ds(m * half, half)
            return pltpu.make_async_copy(act_h.at[:, cols], act_v.at[:, cols], ld.at[m])
        def load_a():
            return pltpu.make_async_copy(a_h, a_v, ld.at[2])
        def load_dy(j):
            return pltpu.make_async_copy(dy_h.at[:, pl.ds(pl.multiple_of(j * 2 * cd, 2 * cd), 2 * cd)], dy_v.at[lax.rem(j, 2)], ldy.at[lax.rem(j, 2)])
        def load_dg(j, e):
            return pltpu.make_async_copy((dg_h, du_h)[e].at[:, pl.ds(pl.multiple_of(j * cg, cg), cg)], dg_v.at[lax.rem(j, 2), e], ldg.at[lax.rem(j, 2), e])
        load_dy(0).start(); load_act(0).start(); load_act(1).start()
        barrier(p)
        def done_d(j, e, v):
            od[:, pl.ds(pl.multiple_of((2 * j + e) * cd, cd), cd)] = v.astype(bf)
        def done_g(j, e, v):
            (og, ou)[e][:, pl.ds(pl.multiple_of(j * cg, cg), cg)] = v.astype(bf)
        sd = Scatter(p, nd, lagd, bufs[:13], done_d)
        sg = Scatter(p, ng, lag, bufs[13:], done_g)
        load_dy(0).wait(); load_act(0).wait()
        def make_d(j):
            @pl.when(j + 1 < nd)
            def _(): load_dy(j + 1).start()
            @pl.when(j == 0)
            def _(): load_a().start()
            @pl.when(j == nd - 1)
            def _():
                for e in (0, 1): load_dg(0, e).start()
            for m in (0, 1):
                if m == 1:
                    @pl.when(j == 0)
                    def _(): load_act(1).wait()
                val = lax.dot_general(act_v[:, m * half:(m + 1) * half], dy_v[lax.rem(j, 2)], TN, preferred_element_type=f32)
                for e in (0, 1):
                    v = val[:, e * cd:(e + 1) * cd].reshape(chips // 2, 2, Rd, cd).astype(bf)
                    for h in (0, 1):
                        sd.own[sd.slot(j, h), e, m * chips // 2:(m + 1) * chips // 2] = v[:, h]
            sd.send(j)
            @pl.when(j + 1 < nd)
            def _(): load_dy(j + 1).wait()
        def make_g(j):
            @pl.when(j + 1 < ng)
            def _():
                for e in (0, 1): load_dg(j + 1, e).start()
            @pl.when(j == 0)
            def _(): load_a().wait()
            for e in (0, 1):
                load_dg(j, e).wait()
            for e in (0, 1):
                val = lax.dot_general(a_v[...], dg_v[lax.rem(j, 2), e], TN, preferred_element_type=f32)
                v = val.reshape(chips, 2, R, cg).astype(bf)
                for h in (0, 1):
                    sg.own[sg.slot(j, h), e] = v[:, h]
            sg.send(j)
        streams = ((sd, nd, 0, lagd, make_d), (sg, ng, nd, lag, make_g))
        total = max(lo + m + (Scatter.STAGES - 1) * lg for _, m, lo, lg, _ in streams)
        def body(i, _):
            for k in reversed(range(Scatter.STAGES)):
                for s, m, lo, lg, make in streams:
                    j = i - lo - k * lg
                    @pl.when((j >= 0) & (j < m))
                    def _():
                        make(j) if k == 0 else s.stage(k, j)
            return 0
        lax.fori_loop(0, total, body, 0)
    S, V, A, D = jax.ShapeDtypeStruct, pl.BlockSpec(memory_space=pltpu.VMEM), pl.BlockSpec(memory_space=pl.ANY), pltpu.SemaphoreType.DMA
    return pl.pallas_call(
        kernel, name="grads",
        out_shape=[S((R, F), bf), S((R, F), bf), S((Rd, Dm), bf)],
        in_specs=[A] * 5, out_specs=[V] * 3,
        scratch_shapes=[pltpu.VMEM((T, Dm), bf), pltpu.VMEM((T, F), bf), pltpu.VMEM((2, 2, T, cg), bf), pltpu.VMEM((2, T, 2 * cd), bf), D((3,)), D((2, 2)), D((2,)),
                        *scatter_bufs(nd, lagd, side, Rd, cd), *scatter_bufs(ng, lag, side, R, cg)],
        compiler_params=pltpu.CompilerParams(collective_id=cid, has_side_effects=True, vmem_limit_bytes=67043328),
    )(a, act, dgate, dup, dy)


def total(n, part, cid=9):
    def kernel(x_ref, o_ref, got, send, recv):
        me = lax.axis_index("dp")
        sem = pltpu.get_barrier_semaphore()
        def other(k):
            return lax.rem(me + k, n)
        def greet(k, _):
            pl.semaphore_signal(sem, inc=1, device_id={"dp": other(k)}, device_id_type=MESH)
            return 0
        lax.fori_loop(1, n, greet, 0)
        pl.semaphore_wait(sem, n - 1)
        def copy(k, slot):
            return pltpu.make_async_remote_copy(src_ref=x_ref, dst_ref=got.at[slot], send_sem=send.at[k], recv_sem=recv.at[slot], device_id={"dp": other(k)}, device_id_type=MESH)
        def start(k, _):
            copy(k, me).start()
            return 0
        lax.fori_loop(1, n, start, 0)
        got[me] = x_ref[...]
        def wait(k, _):
            copy(k, me).wait_send()
            copy(k, other(k)).wait_recv()
            return 0
        lax.fori_loop(1, n, wait, 0)
        o_ref[...] = jnp.sum(got[...], axis=0)
    V = pl.BlockSpec(memory_space=pltpu.VMEM)
    D = pltpu.SemaphoreType.DMA
    return pl.pallas_call(
        kernel, name="total", out_shape=jax.ShapeDtypeStruct(part.shape, jnp.float32), in_specs=[V], out_specs=V,
        scratch_shapes=[pltpu.VMEM((n, *part.shape), jnp.float32), D((n,)), D((n,))],
        compiler_params=pltpu.CompilerParams(collective_id=cid, has_side_effects=True),
    )(part)


def matmul(a, w):
    return jnp.dot(a, w, preferred_element_type=f32).astype(bf)


def matmul_t(a, w):
    return lax.dot_general(a, w, (((1,), (1,)), ((), ())), preferred_element_type=f32).astype(bf)


def normed(h):
    wide = h.astype(f32)
    scale = lax.rsqrt(jnp.mean(wide**2, -1, keepdims=True) + 1e-6)
    return (wide * scale).astype(bf)


def gated(gate, up):
    return (jax.nn.silu(gate) * up).astype(bf)


def adamw(w, m, v, g):
    m = 0.9 * m + 0.1 * g
    v = 0.95 * v + 0.05 * g * g
    step = m * lax.rsqrt(v + 1e-8) + 0.1 * w
    return (w - 0.02 * step).astype(bf), m, v


def clipped(gradients, sum_of_squares, count):
    factor = jnp.minimum(1.0, 0.5 * lax.rsqrt(sum_of_squares / count + 1e-30))
    return [g * factor for g in gradients]


def solution(mesh):
    n = mesh.shape["dp"]

    def step(x, dy, *arrays):
        weights, m, v = (arrays[i : i + 3] for i in (0, 3, 6))
        layers = weights[0].shape[0]
        wg, wu, wd = gather_all(n, *weights, lag=4, cd=256)
        h, kept = x[0], []
        for l in range(layers):
            a = normed(h)
            gate = jnp.dot(a, wg[l], preferred_element_type=f32)
            up = jnp.dot(a, wu[l], preferred_element_type=f32)
            act, back = jax.vjp(gated, gate, up)
            kept.append((h, a, act, back))
            if l < layers - 1:
                h = h + matmul(act, wd[l])
        by_h, mine = dy[0], [None] * layers
        for l in reversed(range(layers)):
            h, a, act, back = kept[l]
            dgate, dup = (d.astype(bf) for d in back(matmul_t(by_h, wd[l])))
            mine[l] = grads(n, a, act, dgate, dup, by_h, cid=2 + l)
            if l:
                da = matmul_t(dgate, wg[l]) + matmul_t(dup, wu[l])
                by_h = by_h + jax.vjp(normed, h)[1](da)[0]
        gradients = [jnp.stack([mine[l][i] for l in range(layers)]).astype(f32) for i in range(3)]
        part = sum(jnp.sum(g * g) for g in gradients)
        squares = total(n, jnp.broadcast_to(part / 1024, (8, 128)))
        squares = jnp.sum(squares)
        gradients = clipped(gradients, squares, n * sum(g.size for g in gradients))
        new = [adamw(w.astype(f32), m, v, g) for w, m, v, g in zip(weights, m, v, gradients, strict=True)]
        return tuple(one[which] for which in range(3) for one in new)

    states, cut = P(("rep", "dp"), None, None), P(None, "dp", None)
    return jax.shard_map(
        step,
        mesh=mesh,
        in_specs=(states, states) + (cut,) * 9,
        out_specs=(P("rep", "dp", None),) * 9,
        check_vma=False,
    )
```

time: 930 us -> 600 us (0.65)
  waiting for transfers between devices: 486 us -> 0 us
  Pallas kernels: 0 us -> 335 us
  matrix products: 331 us -> 198 us
  blocking collectives: 46.3 us -> 0 us
  between operations: 17.5 us -> 3.96 us
    reduce_scatter x6 -> x0, waiting for transfers between devices: 341 us -> none  [step(): lax.psum_scatter(by_w[name], 'dp', scatter_dimension=0, tiled=True)]
    pallas_call x0 -> x4, Pallas kernels: none -> 335 us  [the longest x2 206 us: grads(): pl.pallas_call(kernel, name='grads', out_shape=[S((R, F), bf), S((R, F),...]
    all_gather x6 -> x0, waiting for transfers between devices: 143 us -> none  [fetched(): lax.all_gather(w[number], 'dp', axis=0, tiled=True)]
    dot_general x15 -> x9, matrix products: 331 us -> 198 us  [the longest x4 87.4 us: matmul_t(): lax.dot_general(a, w, (((1,), (1,)), ((), ())), preferred_element_type=f32)]
    psum x1 -> x0, blocking collectives: 46.3 us -> none  [step(): squares = lax.psum(sum((jnp.sum(g * g) for g in gradients)), 'dp')]
    slice x3 -> x2, local copies, waits for them, and re-layouts: 5.29 us -> 25.4 us  [the longest x1 14.3 us: step(): gate = jnp.dot(a, wg[l], preferred_element_type=f32)]
    unnamed x32 -> x38, local copies, waits for them, and re-layouts: 15.1 us -> 3.03 us
  transfers between devices with their start and end apart: 12 -> 0, of which waited for: 11 -> 0; matrix products, arithmetic and copies ran while one was open for 29% -> 0% of each run, Pallas kernels for 0% -> 0%
where the time goes in v1:
time: 600 us; the launch traced here: 592 us
  Pallas kernels  335 us (56%)
  matrix products  198 us (33%)
  local copies, waits for them, and re-layouts  29 us (5%)
  other arithmetic  26.7 us (4%)
    pallas_call x2, Pallas kernels, grads(): pl.pallas_call(kernel, name='grads', out_shape=[S((R, F), bf), S((R, F),...  206 us
    pallas_call x1, Pallas kernels, gather_all(): pl.pallas_call(kernel, name='gather', out_shape=[S((L, side, side, 2, R,...  112 us
    dot_general x4, matrix products, matmul_t(): lax.dot_general(a, w, (((1,), (1,)), ((), ())), preferred_element_type=f32)  87.4 us
    dot_general x2, matrix products, step(): gate = jnp.dot(a, wg[l], preferred_element_type=f32)  50.4 us
    dot_general x2, matrix products, step(): up = jnp.dot(a, wu[l], preferred_element_type=f32)  42.5 us
    dot_general x1, matrix products, matmul(): return jnp.dot(a, w, preferred_element_type=f32).astype(bf)  17.6 us
    pallas_call x1, Pallas kernels, total(): pl.pallas_call(kernel, name='total', out_shape=jax.ShapeDtypeStruct(part....  16.5 us
    slice x1, local copies, waits for them, and re-layouts, step(): gate = jnp.dot(a, wg[l], preferred_element_type=f32)  14.3 us

profile of v1, /device:TPU:97, one launch (start us, length us, event | category | flops | bytes accessed | tf_op | source)
XLA Modules:
  0.0 592.5 jit_solution(858384343819781789)
XLA Ops:
  3.6 112.4 %gather.1 = (bf16[2,4,4,2,32,2816]{5,4,3,2,1,0:T(8,128)(2,1)}, bf16[2,4,4,2,32,2816]{5,4,3,2,1,0:T(8,128)(2,1)}, bf16[2,4,4,2,88,1024]{5,4,3,2,1,0:T(8,128)(2,1)}) custom-call(bf16[2,32,2816]{2,1,0:T(8,128)(2,1)S(1)} %copy-done.2, bf16[2,32,2816]{2,1,0:T(8,128)(2,1)S(1)} %copy-done.1, bf16[2,88,1024]{2,1,0:T(8,128)(2,1)S(1)} %copy-done), custom_call_target="tpu_custom_call" | custom-call | tf_op jit(solution)/shard_map/gather/pallas_call | solution.py:150
  116.0 14.3 %fusion.53 = (bf16[1,4,4,2,32,2816]{5,4,3,2,1,0:T(8,128)(2,1)}, bf16[1,4,4,2,32,2816]{5,4,3,2,1,0:T(8,128)(2,1)S(1)}, bf16[1,4,4,2,32,2816]{5,4,3,2,1,0:T(8,128)(2,1)}, bf16[1,4,4,2,32,2816]{5,4,3,2,1,0:T(8,128)(2,1)}) fusion(bf16[2,4,4,2,32,2816]{5,4,3,2,1,0:T(8,128)(2,1)} %get-tuple-element.18, bf16[2,4,4,2,32,2816]{5,4,3,2,1,0:T(8,128)(2,1)} %get-tuple-element.19), kind=kLoop, calls=%fused_computation.88 | loop fusion | bytes 46137344 | tf_op jit(solution)/shard_map/slice | solution.py:394
  131.3 15.7 %fusion.21 = f32[2048,2816]{1,0:T(8,128)} fusion(bf16[1024,2816]{1,0:T(8,128)(2,1)S(1)} %bitcast.59, bf16[1,2048,1024]{2,1,0:T(8,128)(2,1)S(1)} %copy-done.4, f32[2048]{0:T(1024)S(1)} %add_rsqrt_fusion), kind=kOutput, calls=%fused_computation.42 | convolution fusion | flops 11817451520 | bytes 33038336 | tf_op jit(solution)/shard_map/dot_general | solution.py:394
  147.0 26.9 %multiply_convert_fusion.1 = (bf16[2048,2816]{1,0:T(8,128)(2,1)}, f32[2048,2816]{1,0:T(8,128)}) fusion(f32[2048,2816]{1,0:T(8,128)} %fusion.21, bf16[1024,2816]{1,0:T(8,128)(2,1)} %bitcast.57, bf16[1,2048,1024]{2,1,0:T(8,128)(2,1)S(1)} %copy-done.4, f32[2048]{0:T(1024)S(1)} %add_rsqrt_fusion), kind=kOutput, calls=%fused_computation.17 | convolution fusion | flops 11852054528 | bytes 67641344 | tf_op jit(solution)/shard_map/dot_general | solution.py:395
  173.9 11.1 %fusion.52 = (bf16[1,4,4,2,88,1024]{5,4,3,2,1,0:T(8,128)(2,1)}, bf16[1,4,4,2,88,1024]{5,4,3,2,1,0:T(8,128)(2,1)}) fusion(bf16[2,4,4,2,88,1024]{5,4,3,2,1,0:T(8,128)(2,1)} %get-tuple-element.20), kind=kLoop, calls=%fused_computation.87 | loop fusion | bytes 23068672 | tf_op jit(solution)/shard_map/slice | solution.py:403
  185.0 17.6 %fusion.14 = (f32[2048]{0:T(1024)S(1)}, bf16[2048,1024]{1,0:T(8,128)(2,1)S(1)}) fusion(bf16[2048,2816]{1,0:T(8,128)(2,1)} %get-tuple-element.47.act_h, bf16[2816,1024]{1,0:T(8,128)(2,1)} %bitcast.49, bf16[1,2048,1024]{2,1,0:T(8,128)(2,1)} %param.11), kind=kOutput, calls=%fused_computation.33 | convolution fusion | flops 11821643776 | bytes 25698304 | tf_op jit(solution)/shard_map/dot_general | solution.py:355
  203.5 15.6 %fusion.55 = f32[2048,2816]{1,0:T(8,128)} fusion(bf16[2048,1024]{1,0:T(8,128)(2,1)S(1)} %fusion.15.a_h, bf16[1024,2816]{1,0:T(8,128)(2,1)S(1)} %bitcast.54), kind=kOutput, calls=%fused_computation.90 | convolution fusion | flops 11811160064 | bytes 33030144 | tf_op jit(solution)/shard_map/dot_general | solution.py:395
  219.1 17.1 %convolution_convert_fusion.1 = bf16[2816,2048]{0,1:T(8,128)(2,1)} fusion(bf16[2816,1024]{1,0:T(8,128)(2,1)} %bitcast.58, bf16[1,2048,1024]{2,1,0:T(8,128)(2,1)S(1)} %copy-done.5), kind=kOutput, calls=%fused_computation.25 | convolution fusion | flops 11816927232 | bytes 21495808 | tf_op jit(solution)/shard_map/dot_general | solution.py:359
  236.2 34.6 %fusion.3 = (bf16[2048,2816]{1,0:T(8,128)(2,1)}, bf16[2048,2816]{1,0:T(8,128)(2,1)}, bf16[2048,2816]{1,0:T(8,128)(2,1)}) fusion(f32[2048,2816]{1,0:T(8,128)} %fusion.55, bf16[2816,2048]{0,1:T(8,128)(2,1)} %convolution_convert_fusion.1, bf16[2048,1024]{1,0:T(8,128)(2,1)} %copy-done.6, bf16[1024,2816]{1,0:T(8,128)(2,1)} %bitcast.55), kind=kOutput, calls=%fused_computation.7 | convolution fusion | flops 11909201920 | bytes 79167488 | tf_op jit(solution)/shard_map/dot_general | solution.py:394
  270.8 17.5 %fusion.56 = bf16[2048,1024]{1,0:T(8,128)(2,1)} fusion(bf16[2048,2816]{1,0:T(8,128)(2,1)} %get-tuple-element.36.dg_h, bf16[1024,2816]{1,0:T(8,128)(2,1)} %bitcast.56), kind=kOutput, calls=%fused_computation.91 | convolution fusion | flops 11811160064 | bytes 21495808 | tf_op jit(solution)/shard_map/dot_general | solution.py:359
  288.3 19.2 %fusion.16 = (f32[2048]{0:T(1024)S(1)}, bf16[2048,1024]{1,0:T(8,128)(2,1)}) fusion(bf16[2048,1024]{1,0:T(8,128)(2,1)S(1)} %get-tuple-element.50, bf16[2048,1024]{1,0:T(8,128)(2,1)} %fusion.56, bf16[2048,2816]{1,0:T(8,128)(2,1)} %get-tuple-element.40.du_h, bf16[1024,2816]{1,0:T(8,128)(2,1)} %bitcast.51), kind=kOutput, calls=%fused_computation.35 | convolution fusion | flops 11823740928 | bytes 29892608 | tf_op jit(solution)/shard_map/dot_general | solution.py:359
  307.5 5.9 %fusion.18.dy_h = bf16[2048,1024]{1,0:T(8,128)(2,1)} fusion(bf16[2048,1024]{1,0:T(8,128)(2,1)S(1)} %get-tuple-element.50, bf16[2048,1024]{1,0:T(8,128)(2,1)} %get-tuple-element.52, f32[2048]{0:T(1024)S(1)} %multiply_multiply_fusion.3, f32[2048]{0:T(1024)S(1)} %copy-done.12, bf16[1,2048,1024]{2,1,0:T(8,128)(2,1)} %param.12), kind=kLoop, calls=%fused_computation.38 | loop fusion | flops 14680064 | bytes 16793600 | tf_op jit(solution)/shard_map/add | solution.py:407
  313.5 33.6 %fusion = (bf16[2048,2816]{1,0:T(8,128)(2,1)}, bf16[2048,2816]{1,0:T(8,128)(2,1)}) fusion(f32[2048,2816]{1,0:T(8,128)} %fusion.21, f32[2048,2816]{1,0:T(8,128)} %get-tuple-element.48, bf16[2048,1024]{1,0:T(8,128)(2,1)} %fusion.18.dy_h, bf16[2816,1024]{1,0:T(8,128)(2,1)} %bitcast.50), kind=kOutput, calls=%fused_computation.4 | convolution fusion | flops 11903434752 | bytes 79167488 | tf_op jit(solution)/shard_map/dot_general | solution.py:359
  347.1 4.9 fusion.11.a_h
  352.0 100.6 %grads.2 = (bf16[32,2816]{1,0:T(8,128)(2,1)}, bf16[32,2816]{1,0:T(8,128)(2,1)}, bf16[88,1024]{1,0:T(8,128)(2,1)}) custom-call(bf16[2048,1024]{1,0:T(8,128)(2,1)} %fusion.11.a_h, bf16[2048,2816]{1,0:T(8,128)(2,1)} %get-tuple-element.47.act_h, bf16[2048,2816]{1,0:T(8,128)(2,1)} %get-tuple-element.39.dg_h, bf16[2048,2816]{1,0:T(8,128)(2,1)} %get-tuple-element.38.du_h, ...), custom_call_target="tpu_custom_call" | custom-call | tf_op jit(solution)/shard_map/grads/pallas_call | solution.py:311
  452.5 105.5 %grads.3 = (bf16[32,2816]{1,0:T(8,128)(2,1)}, bf16[32,2816]{1,0:T(8,128)(2,1)}, bf16[88,1024]{1,0:T(8,128)(2,1)}) custom-call(bf16[2048,1024]{1,0:T(8,128)(2,1)} %copy-done.6, bf16[2048,2816]{1,0:T(8,128)(2,1)} %get-tuple-element.37.act_h, bf16[2048,2816]{1,0:T(8,128)(2,1)} %get-tuple-element.36.dg_h, bf16[2048,2816]{1,0:T(8,128)(2,1)} %get-tuple-element.40.du_h, ...), custom_call_target="tpu_custom_call" | custom-call | tf_op jit(solution)/shard_map/grads/pallas_call | solution.py:311
  558.1 1.9 fusion.34
  560.0 1.8 fusion.33
  561.8 1.8 fusion.32
  566.1 16.5 %total.1 = f32[8,128]{1,0:T(8,128)} custom-call(f32[8,128]{1,0:T(8,128)} %broadcast_in_dim.2.x_ref), custom_call_target="tpu_custom_call" | custom-call | tf_op jit(solution)/shard_map/total/pallas_call | solution.py:347
  582.6 1.3 reduce_sum.77
  584.6 3.0 fusion.40
  587.6 3.0 fusion.37
  590.6 1.4 fusion.31
  (45 shorter events, 5.3 us)
Async XLA Ops:
  0.6 1.0 copy-start
  1.6 1.0 copy-start.1
  2.6 1.0 copy-start.2
  116.0 14.3 %copy-start.4 = (bf16[1,2048,1024]{2,1,0:T(8,128)(2,1)S(1)}, bf16[1,2048,1024]{2,1,0:T(8,128)(2,1)}, u32[]{:S(2)}) copy-start(bf16[1,2048,1024]{2,1,0:T(8,128)(2,1)} %param.11) | copy-start | bytes 12582916
  131.2 15.8 %copy-start.13 = (f32[2048]{0:T(1024)}, f32[2048]{0:T(1024)S(1)}, u32[]{:S(2)}) copy-start(f32[2048]{0:T(1024)S(1)} %add_rsqrt_fusion) | copy-start | bytes 24580
  185.0 18.4 %slice-start = ((s8[5767168]{0:T(1024)(128)(4,1)}), s8[4194304]{0:T(1024)(128)(4,1)S(1)}, s32[]{:S(2)}) async-start(s8[5767168]{0:T(1024)(128)(4,1)} %bitcast.52), calls=%async_computation | async-start | bytes 8388608
  185.0 18.5 %slice-start.1 = ((s8[5767168]{0:T(1024)(128)(4,1)}), s8[1572864]{0:T(1024)(128)(4,1)S(1)}, s32[]{:S(2)}) async-start(s8[5767168]{0:T(1024)(128)(4,1)} %bitcast.52), calls=%async_computation.1 | async-start | bytes 3145728
  202.7 16.4 %copy-start.15 = (f32[2048]{0:T(1024)}, f32[2048]{0:T(1024)S(1)}, u32[]{:S(2)}) copy-start(f32[2048]{0:T(1024)S(1)} %get-tuple-element.49) | copy-start | bytes 24580
  202.7 16.4 %copy-start.11 = (f32[2048]{0:T(1024)}, f32[2048]{0:T(1024)S(1)}, u32[]{:S(2)}) copy-start(f32[2048]{0:T(1024)S(1)} %fusion.44) | copy-start | bytes 24580
  203.4 15.6 %copy-start.6 = (bf16[2048,1024]{1,0:T(8,128)(2,1)}, bf16[2048,1024]{1,0:T(8,128)(2,1)S(1)}, u32[]{:S(2)}) copy-start(bf16[2048,1024]{1,0:T(8,128)(2,1)S(1)} %fusion.15.a_h) | copy-start | bytes 12582916
  203.5 15.6 %copy-start.5 = (bf16[1,2048,1024]{2,1,0:T(8,128)(2,1)S(1)}, bf16[1,2048,1024]{2,1,0:T(8,128)(2,1)}, u32[]{:S(2)}) copy-start(bf16[1,2048,1024]{2,1,0:T(8,128)(2,1)} %param.12) | copy-start | bytes 12582916
  288.3 19.2 %copy-start.16 = (f32[2048]{0:T(1024)S(1)}, f32[2048]{0:T(1024)}, u32[]{:S(2)}) copy-start(f32[2048]{0:T(1024)} %copy-done.15) | copy-start | bytes 24580
  288.3 19.2 %copy-start.12 = (f32[2048]{0:T(1024)S(1)}, f32[2048]{0:T(1024)}, u32[]{:S(2)}) copy-start(f32[2048]{0:T(1024)} %copy-done.11) | copy-start | bytes 24580
  313.4 33.6 %copy-start.14 = (f32[2048]{0:T(1024)S(1)}, f32[2048]{0:T(1024)}, u32[]{:S(2)}) copy-start(f32[2048]{0:T(1024)} %copy-done.13) | copy-start | bytes 24580
  558.0 32.6 %copy-start.3 = (bf16[2,32,2816]{2,1,0:T(8,128)(2,1)S(1)}, bf16[2,32,2816]{2,1,0:T(8,128)(2,1)}, u32[]{:S(2)}) copy-start(bf16[2,32,2816]{2,1,0:T(8,128)(2,1)} %wg_ref.1) | copy-start | bytes 1081348
  558.0 32.6 %copy-start.7 = (bf16[32,2816]{1,0:T(8,128)(2,1)S(1)}, bf16[32,2816]{1,0:T(8,128)(2,1)}, u32[]{:S(2)}) copy-start(bf16[32,2816]{1,0:T(8,128)(2,1)} %get-tuple-element.21) | copy-start | bytes 540676
  558.0 32.6 %copy-start.8 = (bf16[32,2816]{1,0:T(8,128)(2,1)S(1)}, bf16[32,2816]{1,0:T(8,128)(2,1)}, u32[]{:S(2)}) copy-start(bf16[32,2816]{1,0:T(8,128)(2,1)} %get-tuple-element.22) | copy-start | bytes 540676
  558.0 32.6 %copy-start.9 = (f32[2,32,2816]{2,1,0:T(8,128)S(1)}, f32[2,32,2816]{2,1,0:T(8,128)}, u32[]{:S(2)}) copy-start(f32[2,32,2816]{2,1,0:T(8,128)} %param.19) | copy-start | bytes 2162692
  558.0 32.6 %copy-start.10 = (f32[2,32,2816]{2,1,0:T(8,128)S(1)}, f32[2,32,2816]{2,1,0:T(8,128)}, u32[]{:S(2)}) copy-start(f32[2,32,2816]{2,1,0:T(8,128)} %param.16) | copy-start | bytes 2162692

commit v2 on v0

v2 whole, which is shorter than its diff:
```python
import functools, math
import jax, jax.numpy as jnp
from jax import lax
from jax.experimental import pallas as pl
from jax.experimental.pallas import tpu as pltpu
from jax.sharding import PartitionSpec as P
MESH = pl.DeviceIdType.MESH
bf = jnp.bfloat16

class Place:
    def __init__(self, n):
        self.side = side = math.isqrt(n // 2)
        me = lax.axis_index("dp")
        self.c = c = lax.rem(me, 2)
        chip = me // 2
        x, y = chip // side, lax.rem(chip, side)
        self.i1 = x + c * (y - x)
        self.i2 = y + c * (x - y)
        self.m1 = side + c * (1 - side)
        self.m2 = 1 + c * (side - 1)
        self.partner = me + 1 - 2 * c
    def mod(self, a):
        return lax.rem(a + 2 * self.side, self.side)
    def chip(self, j1, j2):
        return j1 * self.m1 + j2 * self.m2
    def next1(self, d):
        return 2 * self.chip(self.mod(self.i1 + d), self.i2) + self.c
    def next2(self, d):
        return 2 * self.chip(self.i1, self.mod(self.i2 + d)) + self.c

def barrier(p):
    sem = pltpu.get_barrier_semaphore()
    others = [p.partner, p.next1(1), p.next1(-1), p.next2(1), p.next2(-1)]
    for o in others:
        pl.semaphore_signal(sem, inc=1, device_id={"dp": o}, device_id_type=MESH)
    pl.semaphore_wait(sem, len(others))

DIRS = (1, -1)
BOTH = (0, 1)

class Gather:
    STAGES = 6

    def __init__(self, p, own, block, row, core, sent, local, sems):
        self.p, self.own, self.block, self.row, self.core, self.sent, self.local = p, own, block, row, core, sent, local
        self.sl, self.s, self.sd, self.r, self.rd = sems

    def remote(self, src, dst, s, r, dev):
        return pltpu.make_async_remote_copy(src_ref=src, dst_ref=dst, send_sem=s, recv_sem=r, device_id={"dp": dev}, device_id_type=MESH)

    def copy(self, k, j, e, core=0):
        p, d = self.p, DIRS[e]
        if k < 2:
            here = self.block(j, e, p.mod(p.i1 - d), p.i2) if k else self.block(j, None, p.i1, p.i2)
            src, to = here if k else self.own(j), p.next1(d)
        else:
            src = here = self.row(j, e, core, p.mod(p.i2 - d)) if k == 3 else self.row(j, None, core, p.i2)
            to = p.next2(d)
        return self.remote(src, here, self.s.at[k, e], self.r.at[j, k, e], to)

    def across(self, j, core):
        g = self.core(j, core)
        return self.remote(g, g, self.sd, self.rd.at[j], self.p.partner)

    def copies(self):
        return [pltpu.make_async_copy(a, b, self.sl.at[k]) for k, (a, b) in enumerate(self.local)]

    def begin(self):
        for c in self.copies():
            c.start()

    def stage(self, k, j):
        if k == self.STAGES - 1:
            self.across(j, 1 - self.p.c).wait_recv()
            return
        if k:
            for e in BOTH:
                self.copy(k - 1, j, e).wait_recv()
        if k < 2:
            for e in BOTH:
                self.copy(k, j, e).start()
        elif k < 4:
            if k == 2:
                @pl.when(j == 0)
                def _():
                    for c in self.copies():
                        c.wait()
            for core in BOTH:
                @pl.when(self.p.c == core)
                def _():
                    for e in BOTH:
                        self.copy(k, j, e, core).start()
        else:
            self.across(j, self.p.c).start()

    def end(self):
        *kinds, across = self.sent
        for k, view in enumerate(kinds):
            for e in BOTH:
                pltpu.make_async_copy(view, view, self.s.at[k, e]).wait()
        pltpu.make_async_copy(across, across, self.sd).wait()


def gather_sems(m, local):
    D = pltpu.SemaphoreType.DMA
    return [D((local,)), D((4, 2)), D, D((m, 4, 2)), D((m,))]


f32 = jnp.float32
TN = (((0,), (0,)), ((), ()))
NT = (((1,), (1,)), ((), ()))


class Scatter:
    STAGES = 6

    def __init__(self, p, lag, bufs, done):
        self.p, self.done = p, done
        self.own, self.q, self.mid, *self.bufs, self.sd, self.rd, self.s, self.r = bufs
        self.keep, self.pool = scatter_slots(self.q.shape[0], lag)

    def remote(self, src, dst, s, r, dev):
        return pltpu.make_async_remote_copy(src_ref=src, dst_ref=dst, send_sem=s, recv_sem=r, device_id={"dp": dev}, device_id_type=MESH)

    def slot(self, j, h):
        mine, other = lax.rem(j, self.keep), self.keep + lax.rem(j, self.pool)
        return mine + (other - mine) * (self.p.c + h - 2 * self.p.c * h)

    def across(self, j):
        return self.remote(self.own.at[self.keep + lax.rem(j, self.pool)], self.q.at[j], self.sd.at[j], self.rd.at[j], self.p.partner)

    def out(self, k):
        return self.bufs[2 * k]

    def got(self, k):
        return self.bufs[2 * k + 1]

    def at(self, j, ref):
        return lax.rem(j, ref.shape[0])

    def copy(self, k, j, e):
        to = self.p.next1(DIRS[e]) if k < 2 else self.p.next2(DIRS[e])
        return self.remote(self.out(k).at[self.at(j, self.out(k)), e], self.got(k).at[j, e], self.s.at[j, k, e], self.r.at[j, k, e], to)

    def send(self, j):
        self.across(j).start()

    def mine(self, j, e, j1, b):
        at = self.p.chip(j1, b)
        return self.own[lax.rem(j, self.keep), e, at].astype(f32) + self.q[j, e, at].astype(f32)

    def stage(self, k, j):
        p, n = self.p, self.p.side
        for c in [self.across(j)] if k == 1 else [self.copy(k - 2, j, e) for e in BOTH]:
            c.wait_recv()
            c.wait_send()
        m = self.at(j, self.mid)
        if k < 5:
            o, out = self.out(k - 1), self.at(j, self.out(k - 1))
        if k == 1:
            for e in BOTH:
                for b in range(n):
                    o[out, e, 0, b] = self.mine(j, e, p.mod(p.i1 + 2), b).astype(bf)
                    o[out, e, 1, b] = self.mine(j, 1 - e, p.mod(p.i1 + DIRS[e]), b).astype(bf)
        elif k == 2:
            for e in BOTH:
                for b in range(n):
                    o[out, e, b] = (self.got(0)[j, e, 0, b].astype(f32) + self.mine(j, e, p.mod(p.i1 + DIRS[e]), b)).astype(bf)
        elif k == 3:
            for h in BOTH:
                for b in range(n):
                    self.mid[m, h, b] = self.got(1)[j, h, b].astype(f32) + self.got(0)[j, 1 - h, 1, b].astype(f32) + self.mine(j, h, p.i1, b)
            for e in BOTH:
                o[out, e, 0] = self.mid[m, e, p.mod(p.i2 + 2)].astype(bf)
                o[out, e, 1] = self.mid[m, 1 - e, p.mod(p.i2 + DIRS[e])].astype(bf)
        elif k == 4:
            for e in BOTH:
                o[out, e] = (self.got(2)[j, e, 0].astype(f32) + self.mid[m, e, p.mod(p.i2 + DIRS[e])]).astype(bf)
        else:
            for h in BOTH:
                self.done(j, h, self.got(3)[j, h].astype(f32) + self.got(2)[j, 1 - h, 1].astype(f32) + self.mid[m, h, p.i2])
        if k < 5:
            for e in BOTH:
                self.copy(k - 1, j, e).start()


def scatter_slots(m, lag):
    return min(m, 3 * lag), min(m, lag + 1)


def scatter_bufs(m, lag, side, R, C):
    keep, pool = scatter_slots(m, lag)
    few, V, D = min(m, lag + 1), pltpu.VMEM, pltpu.SemaphoreType.DMA
    pairs = [V((k, 2, *s, R, C), bf) for s in ((2, side), (side,), (2,), ()) for k in (few, m)]
    return [V((keep + pool, 2, side * side, R, C), bf), V((m, 2, side * side, R, C), bf), V((min(m, 2 * lag + 1), 2, side, R, C), f32), *pairs,
            D((m,)), D((m,)), D((m, 4, 2)), D((m, 4, 2))]


def normed_rows(h):
    wide = h.astype(f32)
    scale = lax.rsqrt(jnp.mean(wide * wide, -1, keepdims=True) + 1e-6)
    return (wide * scale).astype(bf)


def forward(n, x, dy, wg, wu, wd, lag=3, cg=256, cd=128, cid=1):
    side = math.isqrt(n // 2)
    T, Dm = x.shape
    L, R, F = wg.shape
    Rd = wd.shape[1]
    ng, nd, rows, tile = F // cg, Dm // (2 * cd), T // 2, T // 8
    width = 2 * cd

    def kernel(x_h, dy_h, wg_ref, wu_ref, wd_ref, ogu, od, g0, u0, act0, h1, a0, a1, act1, dg1, du1,
               xv, av, dyv, actv, own_v, wb, wdb, wdr, stg, st3, s_in, s_w, s_wd, s_wr, s_stg, s_act, s_out, s_st3, *sems):
        p = Place(n)
        pltpu.make_async_copy(x_h, xv, s_in.at[0]).start()
        pltpu.make_async_copy(dy_h, dyv, s_in.at[1]).start()
        own_v[:, 0] = wg_ref[...]
        own_v[:, 1] = wu_ref[...]
        barrier(p)
        every = slice(None)

        def cols(j, w):
            return pl.ds(pl.multiple_of(j * w, w), w)
        def core_rows(c):
            return pl.ds(c * Rd if isinstance(c, int) else pl.multiple_of(c * Rd, 8), Rd)
        def place(q, m):
            return q // m, lax.rem(q, m)

        def at_g(q, e, x, y, c):
            l, j = place(q, ng)
            return ogu.at[l, x, y, c, every if e is None else e, every, cols(j, cg)]
        def at_d(q, e, x, y, c):
            l, j = place(q, nd)
            return od.at[l, x, y, core_rows(c), cols(j, width) if e is None else cols(2 * j + e, cd)]
        def own_g(q):
            l, j = place(q, ng)
            return own_v.at[l, every, every, cols(j, cg)]
        def own_d(q):
            l, j = place(q, nd)
            return wd_ref.at[l, every, cols(j, width)]

        def stream(at, own, sent, local, sems):
            x, y = p.i1 + p.c * (p.i2 - p.i1), p.i2 + p.c * (p.i1 - p.i2)
            def block(q, e, j1, j2):
                return at(q, e, j1 + p.c * (j2 - j1), j2 + p.c * (j1 - j2), p.c)
            def row(q, e, core, j2):
                return at(q, e, j2, every, core) if core else at(q, e, every, j2, core)
            def core(q, c):
                return at(q, None, every, every, c)
            return Gather(p, own, block, row, core, sent, local(x, y), sems)

        r0, h0 = core_rows(0), pl.ds(0, Dm // 2)
        sent_g = [ogu.at[:, 0, 0, 0], ogu.at[:, 0, 0, 0, 0], ogu.at[:, :, 0, 0], ogu.at[:, :, 0, 0, 0], ogu.at[:, :, :, 0]]
        sent_d = [od.at[:, 0, 0, r0], od.at[:, 0, 0, r0, h0], od.at[:, :, 0, r0], od.at[:, :, 0, r0, h0], od.at[:, :, :, r0]]
        G = stream(at_g, own_g, sent_g, lambda x, y: [(own_v.at[l], ogu.at[l, x, y, p.c]) for l in range(L)], sems[:5])
        Ds = stream(at_d, own_d, sent_d, lambda x, y: [(wd_ref.at[l], od.at[l, x, y, core_rows(p.c)]) for l in range(L)], sems[5:])
        G.begin()
        Ds.begin()
        downs = 2 * nd
        chunks, depth = 2 * ng + downs, (Gather.STAGES - 1) * lag

        def load_g(q):
            l, j = place(q, ng)
            return pltpu.make_async_copy(ogu.at[l, :, :, :, :, :, cols(j, cg)], wb.at[lax.rem(q, 2)], s_w.at[lax.rem(q, 2)])
        def load_d(j):
            return pltpu.make_async_copy(od.at[0, :, :, :, cols(j, width)], wdb.at[lax.rem(j, 2)], s_wd.at[lax.rem(j, 2)])
        def load_r(k):
            return pltpu.make_async_copy(od.at[1, k // side, lax.rem(k, side)], wdr.at[pl.ds(pl.multiple_of(k * 2 * Rd, 2 * Rd), 2 * Rd)], s_wr.at[k])
        def weights(q, e):
            return wb[lax.rem(q, 2), :, :, :, e].reshape(Dm, cg)
        def part(r):
            return pl.ds(pl.multiple_of(r * rows, rows), rows)
        def put_g(j, r):
            return [pltpu.make_async_copy(stg.at[r, e], (g0, u0)[e].at[part(r), cols(j, cg)], s_stg.at[r, e]) for e in BOTH]
        def put_act(j):
            return pltpu.make_async_copy(actv.at[:, cols(j, cg)], act0.at[:, cols(j, cg)], s_act.at[j])
        def put_3(j, r):
            return [pltpu.make_async_copy(st3.at[r, e], (act1, dg1, du1)[e].at[part(r), cols(j, cg)], s_st3.at[r, e]) for e in (0, 1, 2)]
        put_a0 = pltpu.make_async_copy(av, a0, s_out.at[0])
        put_h1 = pltpu.make_async_copy(xv, h1, s_out.at[1])
        put_a1 = pltpu.make_async_copy(av, a1, s_out.at[2])

        def norm():
            def one(r, _):
                rs_ = pl.ds(pl.multiple_of(r * tile, tile), tile)
                av[rs_, :] = normed_rows(xv[rs_, :])
                return 0
            lax.fori_loop(0, T // tile, one, 0)

        def first():
            pltpu.make_async_copy(x_h, xv, s_in.at[0]).wait()
            pltpu.make_async_copy(dy_h, dyv, s_in.at[1]).wait()
            norm()
            put_a0.start()

        def gate_up(j):
            load_g(j).wait()
            def one(r, _):
                @pl.when(j > 0)
                def _():
                    for c in put_g(j - 1, r):
                        c.wait()
                a = av[part(r), :]
                g = jnp.dot(a, weights(j, 0), preferred_element_type=f32)
                u = jnp.dot(a, weights(j, 1), preferred_element_type=f32)
                stg[r, 0] = g
                stg[r, 1] = u
                actv[part(r), cols(j, cg)] = (g * jax.nn.sigmoid(g) * u).astype(bf)
                for c in put_g(j, r):
                    c.start()
                return 0
            lax.fori_loop(0, 2, one, 0)
            put_act(j).start()

        def down(j):
            load_d(j).wait()
            def one(r, _):
                y = jnp.dot(actv[part(r), :], wdb[lax.rem(j, 2)].reshape(F, width), preferred_element_type=f32).astype(bf)
                xv[part(r), cols(j, width)] = xv[part(r), cols(j, width)] + y
                return 0
            lax.fori_loop(0, 2, one, 0)

        def second():
            for r in BOTH:
                for c in put_g(ng - 1, r):
                    c.wait()
            put_a0.wait()
            put_h1.start()
            norm()
            put_a1.start()

        def gate_up_back(j):
            load_g(ng + j).wait()
            @pl.when(j == 0)
            def _():
                def wait(k, _):
                    load_r(k).wait()
                    return 0
                lax.fori_loop(0, side * side, wait, 0)
            def one(r, _):
                @pl.when(j > 0)
                def _():
                    for c in put_3(j - 1, r):
                        c.wait()
                a = av[part(r), :]
                g = jnp.dot(a, weights(ng + j, 0), preferred_element_type=f32)
                u = jnp.dot(a, weights(ng + j, 1), preferred_element_type=f32)
                d = lax.dot_general(dyv[part(r), :], wdr[cols(j, cg), :], NT, preferred_element_type=f32).astype(bf).astype(f32)
                s = jax.nn.sigmoid(g)
                gs = g * s
                st3[r, 0] = (gs * u).astype(bf)
                st3[r, 1] = (d * u * (s + gs * (1.0 - s))).astype(bf)
                st3[r, 2] = (d * gs).astype(bf)
                for c in put_3(j, r):
                    c.start()
                return 0
            lax.fori_loop(0, 2, one, 0)

        def tick(t, _):
            for k in reversed(range(Gather.STAGES)):
                q = t - k * lag
                late = q >= ng + downs
                @pl.when((q >= 0) & (q < chunks) & ((q < ng) | late))
                def _():
                    j = q - jnp.where(late, downs, 0)
                    G.stage(k, j)
                    if k == Gather.STAGES - 1:
                        load_g(j).start()
                @pl.when((q >= ng) & (q < ng + downs))
                def _():
                    j = q - ng
                    Ds.stage(k, j)
                    if k == Gather.STAGES - 1:
                        @pl.when(j < nd)
                        def _():
                            load_d(j).start()
                        @pl.when(j == downs - 1)
                        def _():
                            def start(k, _):
                                load_r(k).start()
                                return 0
                            lax.fori_loop(0, side * side, start, 0)
            @pl.when(t == min(2, lag - 1))
            def _():
                first()
            m = t - depth - 1
            @pl.when((m >= 0) & (m < ng))
            def _():
                gate_up(m)
            @pl.when((m >= ng) & (m < ng + nd))
            def _():
                down(m - ng)
            @pl.when(m == ng + nd)
            def _():
                second()
            @pl.when(m >= ng + downs)
            def _():
                gate_up_back(m - ng - downs)
            return 0
        lax.fori_loop(0, chunks + depth + 1, tick, 0)
        for r in BOTH:
            for c in put_3(ng - 1, r):
                c.wait()
        G.end()
        Ds.end()
        def last(j, _):
            put_act(j).wait()
            return 0
        lax.fori_loop(0, ng, last, 0)
        put_h1.wait()
        put_a1.wait()

    S, V, A, D = jax.ShapeDtypeStruct, pl.BlockSpec(memory_space=pltpu.VMEM), pl.BlockSpec(memory_space=pl.ANY), pltpu.SemaphoreType.DMA
    VM = pltpu.VMEM
    sems = gather_sems(L * ng, L) + gather_sems(L * nd, L)
    wide, thin = S((T, F), bf), S((T, Dm), bf)
    out = pl.pallas_call(
        kernel, name="forward",
        out_shape=[S((L, side, side, 2, 2, R, F), bf), S((L, side, side, 2 * Rd, Dm), bf),
                   S((T, F), f32), S((T, F), f32), wide, thin, thin, thin, wide, wide, wide],
        in_specs=[A, A, V, V, V], out_specs=[A] * 11,
        scratch_shapes=[VM((T, Dm), bf), VM((T, Dm), bf), VM((T, Dm), bf), VM((T, F), bf), VM((L, 2, R, F), bf), VM((2, side, side, 2, 2, R, cg), bf), VM((2, side, side, 2 * Rd, width), bf), VM((F, Dm), bf),
                        VM((2, 2, rows, cg), f32), VM((2, 3, rows, cg), bf),
                        D((2,)), D((2,)), D((2,)), D((side * side,)), D((2, 2)), D((ng,)), D((3,)), D((2, 3)), *sems],
        compiler_params=pltpu.CompilerParams(collective_id=cid, has_side_effects=True, vmem_limit_bytes=67043328),
    )(x, dy, wg, wu, wd)
    ogu, od, *rest = out
    return ogu, od.reshape(L, n * Rd, Dm), *rest


class Layer:
    def __init__(self, n, a, act, lag, lagd, cg, cd):
        self.n, self.side = n, math.isqrt(n // 2)
        self.T, self.Dm = a.shape
        self.F = act.shape[1]
        self.R, self.Rd, self.ng, self.nd = self.Dm // n, self.F // n, self.F // cg, self.Dm // (2 * cd)
        self.lag, self.lagd, self.cg, self.cd, self.half, self.chips = lag, lagd, cg, cd, self.F // 2, self.side * self.side
    def bufs(self):
        return [*scatter_bufs(self.nd, self.lagd, self.side, self.Rd, self.cd), *scatter_bufs(self.ng, self.lag, self.side, self.R, self.cg)]
    def outs(self):
        S = jax.ShapeDtypeStruct
        return [S((self.R, self.F), bf), S((self.R, self.F), bf), S((self.Rd, self.Dm), bf), S((8, 128), f32)]
    def streams(self, p, og, ou, od, sq, bufs):
        def add(v):
            w = v.astype(f32)
            w = jnp.sum((w * w).reshape(w.shape[0] // 8, 8, w.shape[1]), 0)
            for k in range(w.shape[1] // 128):
                sq[...] += w[:, 128 * k:128 * k + 128]
        def done_d(j, e, v):
            v = v.astype(bf)
            od[:, pl.ds(pl.multiple_of((2 * j + e) * self.cd, self.cd), self.cd)] = v
            add(v)
        def done_g(j, e, v):
            v = v.astype(bf)
            (og, ou)[e][:, pl.ds(pl.multiple_of(j * self.cg, self.cg), self.cg)] = v
            add(v)
        sq[...] = jnp.zeros_like(sq)
        self.p = p
        split = len(bufs) // 2
        self.sd = Scatter(p, self.lagd, bufs[:split], done_d)
        self.sg = Scatter(p, self.lag, bufs[split:], done_g)
    def put_d(self, j, m, val):
        for e in BOTH:
            v = val[:, e * self.cd:(e + 1) * self.cd].reshape(self.chips // 2, 2, self.Rd, self.cd).astype(bf)
            for h in BOTH:
                self.sd.own[self.sd.slot(j, h), e, m * self.chips // 2:(m + 1) * self.chips // 2] = v[:, h]
    def put_g(self, j, val):
        for e in BOTH:
            v = val[:, e * self.cg:(e + 1) * self.cg].reshape(self.chips, 2, self.R, self.cg).astype(bf)
            for h in BOTH:
                self.sg.own[self.sg.slot(j, h), e] = v[:, h]
    def run(self, make_d, make_g, extra=0, more=None):
        streams = ((self.sd, self.nd, 0, self.lagd, make_d), (self.sg, self.ng, self.nd, self.lag, make_g))
        total = max(lo + m + (Scatter.STAGES - 1) * lg for _, m, lo, lg, _ in streams)
        total = max(total, self.nd + self.ng + extra)
        def body(i, _):
            for k in reversed(range(Scatter.STAGES)):
                for s, m, lo, lg, make in streams:
                    j = i - lo - k * lg
                    @pl.when((j >= 0) & (j < m))
                    def _():
                        make(j) if k == 0 else s.stage(k, j)
            if extra:
                j = i - self.nd - self.ng
                @pl.when((j >= 0) & (j < extra))
                def _():
                    more(j)
            return 0
        lax.fori_loop(0, total, body, 0)


def cols_of(j, w):
    return pl.ds(pl.multiple_of(j * w, w), w)


def backward_last(n, a, act, dgate, dup, dy, h, wgu, layer, lag=2, lagd=2, cg=256, cd=128, cid=2):
    k = Layer(n, a, act, lag, lagd, cg, cd)
    T, Dm, F, tile = k.T, k.Dm, k.F, k.T // 8
    def kernel(a_h, act_h, dg_h, du_h, dy_h, h_h, w_h, og, ou, od, sq, dh_h,
               a_v, act_v, dg_v, dy_v, row_v, h_v, y_v, o_v, ld, ldg, ldy, ldr, ldo, ldw, *bufs):
        p = Place(n)
        def load_act(m):
            cols = pl.ds(m * k.half, k.half)
            return pltpu.make_async_copy(act_h.at[:, cols], act_v.at[:T, cols], ld.at[m])
        load_a = pltpu.make_async_copy(a_h, a_v, ld.at[2])
        def load_dy(j):
            return pltpu.make_async_copy(dy_h.at[:, cols_of(j, 2 * cd)], dy_v.at[lax.rem(j, 2)], ldy.at[lax.rem(j, 2)])
        def load_dg(j, e):
            return pltpu.make_async_copy((dg_h, du_h)[e].at[:, cols_of(j, cg)], dg_v.at[lax.rem(j, 2), :, e * cg:(e + 1) * cg], ldg.at[lax.rem(j, 2), e])
        def load_w(d):
            for e in BOTH:
                chip = d // 2
                rows = pl.ds(pl.multiple_of((e * n + d) * k.R, k.R), k.R)
                pltpu.make_async_copy(w_h.at[layer, chip // k.side, lax.rem(chip, k.side), lax.rem(d, 2), e], act_v.at[rows], ldw).start()
            return 0
        w_v = act_v.at[:2 * Dm]
        def load_row(r, e):
            return pltpu.make_async_copy((dg_h, du_h)[e].at[cols_of(r, tile), :], row_v.at[e], ldr.at[e])
        def load_h(r):
            return pltpu.make_async_copy(h_h.at[cols_of(r, tile), :], h_v, ldr.at[2])
        def load_y(r):
            return pltpu.make_async_copy(dy_h.at[cols_of(r, tile), :], y_v, ldr.at[3])
        def put(r):
            return pltpu.make_async_copy(o_v, dh_h.at[cols_of(r, tile), :], ldo)
        load_dy(0).start(); load_act(0).start(); load_act(1).start()
        barrier(p)
        k.streams(p, og, ou, od, sq, bufs)
        load_dy(0).wait(); load_act(0).wait()
        def make_d(j):
            @pl.when(j + 1 < k.nd)
            def _(): load_dy(j + 1).start()
            @pl.when(j == 0)
            def _(): load_a.start()
            @pl.when(j == k.nd - 1)
            def _():
                for e in BOTH: load_dg(0, e).start()
            for m in BOTH:
                if m == 1:
                    @pl.when(j == 0)
                    def _(): load_act(1).wait()
                k.put_d(j, m, lax.dot_general(act_v[:T, m * k.half:(m + 1) * k.half], dy_v[lax.rem(j, 2)], TN, preferred_element_type=f32))
            k.sd.send(j)
            @pl.when(j + 1 < k.nd)
            def _(): load_dy(j + 1).wait()
        def make_g(j):
            @pl.when(j + 1 < k.ng)
            def _():
                for e in BOTH: load_dg(j + 1, e).start()
            @pl.when(j == 0)
            def _():
                lax.fori_loop(0, n, lambda d, _: load_w(d), 0)
                load_a.wait()
            @pl.when(j == k.ng - 1)
            def _():
                for e in BOTH: load_row(0, e).start()
                load_h(0).start(); load_y(0).start()
            for e in BOTH:
                load_dg(j, e).wait()
            k.put_g(j, lax.dot_general(a_v[...], dg_v[lax.rem(j, 2)], TN, preferred_element_type=f32))
            k.sg.send(j)
        def rows(r):
            @pl.when(r == 0)
            def _():
                pltpu.make_async_copy(w_v, w_v, ldw).wait()
            @pl.when(r > 0)
            def _():
                put(r - 1).wait()
            def again(c):
                @pl.when(r + 1 < T // tile)
                def _(): c.start()
            both = []
            for e in BOTH:
                load_row(r, e).wait()
                both.append(lax.dot_general(row_v[e], act_v[e * Dm:(e + 1) * Dm], NT, preferred_element_type=f32).astype(bf))
                again(load_row(r + 1, e))
            da = (both[0] + both[1]).astype(f32)
            load_h(r).wait(); load_y(r).wait()
            wide = h_v[...].astype(f32)
            s = lax.rsqrt(jnp.mean(wide * wide, -1, keepdims=True) + 1e-6)
            t = jnp.sum(da * wide, -1, keepdims=True) * (s * s * s) * (1.0 / Dm)
            o_v[...] = (da * s - wide * t).astype(bf) + y_v[...]
            put(r).start()
            again(load_h(r + 1)); again(load_y(r + 1))
        k.run(make_d, make_g, T // tile, rows)
        put(T // tile - 1).wait()
    V, A, D, VM = pl.BlockSpec(memory_space=pltpu.VMEM), pl.BlockSpec(memory_space=pl.ANY), pltpu.SemaphoreType.DMA, pltpu.VMEM
    return pl.pallas_call(
        kernel, name="backward_last", out_shape=[*k.outs(), jax.ShapeDtypeStruct((T, Dm), bf)], in_specs=[A] * 7, out_specs=[V] * 4 + [A],
        scratch_shapes=[VM((T, Dm), bf), VM((max(T, 2 * Dm), F), bf), VM((2, T, 2 * cg), bf), VM((2, T, 2 * cd), bf), VM((2, tile, F), bf), VM((tile, Dm), bf), VM((tile, Dm), bf), VM((tile, Dm), bf),
                        D((3,)), D((2, 2)), D((2,)), D((4,)), D, D, *k.bufs()],
        compiler_params=pltpu.CompilerParams(collective_id=cid, has_side_effects=True, vmem_limit_bytes=67043328),
    )(a, act, dgate, dup, dy, h, wgu)


def backward_first(n, a, act, gate, up, dh, wd, layer, lag=2, lagd=2, cg=256, cd=128, cid=3):
    k = Layer(n, a, act, lag, lagd, cg, cd)
    T, Dm, F, rows = k.T, k.Dm, k.F, k.T // 2
    def kernel(a_h, act_h, g_h, u_h, dh_h, wd_h, og, ou, od, sq, a_v, act_v, gu_v, dg_v, dh_v, wd_v, ld, ldg, ldw, *bufs):
        p = Place(n)
        def load_act(m):
            cols = pl.ds(m * k.half, k.half)
            return pltpu.make_async_copy(act_h.at[:, cols], act_v.at[:, cols], ld.at[m])
        load_a = pltpu.make_async_copy(a_h, a_v, ld.at[2])
        load_dh = pltpu.make_async_copy(dh_h, dh_v, ld.at[3])
        def part(r):
            return pl.ds(pl.multiple_of(r * rows, rows), rows)
        def load_gu(j, r):
            return [pltpu.make_async_copy((g_h, u_h)[e].at[part(r), cols_of(j, cg)], gu_v.at[r, e], ldg.at[r, e]) for e in BOTH]
        def load_wd(j):
            return pltpu.make_async_copy(wd_h.at[layer, cols_of(j, cg), :], wd_v, ldw)
        load_dh.start(); load_act(0).start(); load_act(1).start()
        barrier(p)
        k.streams(p, og, ou, od, sq, bufs)
        load_dh.wait(); load_act(0).wait()
        def make_d(j):
            @pl.when(j == 0)
            def _(): load_a.start()
            @pl.when(j == k.nd - 1)
            def _():
                for r in BOTH:
                    for c in load_gu(0, r): c.start()
                load_wd(0).start()
            for m in BOTH:
                if m == 1:
                    @pl.when(j == 0)
                    def _(): load_act(1).wait()
                k.put_d(j, m, lax.dot_general(act_v[:, m * k.half:(m + 1) * k.half], dh_v[:, cols_of(j, 2 * cd)], TN, preferred_element_type=f32))
            k.sd.send(j)
        def make_g(j):
            @pl.when(j == 0)
            def _(): load_a.wait()
            load_wd(j).wait()
            def one(r, _):
                for c in load_gu(j, r):
                    c.wait()
                d = lax.dot_general(dh_v[part(r), :], wd_v[...], NT, preferred_element_type=f32).astype(bf).astype(f32)
                g, u = gu_v[r, 0], gu_v[r, 1]
                s = jax.nn.sigmoid(g)
                gs = g * s
                dg_v[part(r), :cg] = (d * u * (s + gs * (1.0 - s))).astype(bf)
                dg_v[part(r), cg:] = (d * gs).astype(bf)
                @pl.when(j + 1 < k.ng)
                def _():
                    for c in load_gu(j + 1, r): c.start()
                return 0
            lax.fori_loop(0, 2, one, 0)
            @pl.when(j + 1 < k.ng)
            def _():
                load_wd(j + 1).start()
            k.put_g(j, lax.dot_general(a_v[...], dg_v[...], TN, preferred_element_type=f32))
            k.sg.send(j)
        k.run(make_d, make_g)
    V, A, D, VM = pl.BlockSpec(memory_space=pltpu.VMEM), pl.BlockSpec(memory_space=pl.ANY), pltpu.SemaphoreType.DMA, pltpu.VMEM
    return pl.pallas_call(
        kernel, name="backward_first", out_shape=k.outs(), in_specs=[A] * 6, out_specs=[V] * 4,
        scratch_shapes=[VM((T, Dm), bf), VM((T, F), bf), VM((2, 2, rows, cg), f32), VM((T, 2 * cg), bf), VM((T, Dm), bf), VM((cg, Dm), bf),
                        D((4,)), D((2, 2)), D, *k.bufs()],
        compiler_params=pltpu.CompilerParams(collective_id=cid, has_side_effects=True, vmem_limit_bytes=67043328),
    )(a, act, gate, up, dh, wd)


def total(n, part, cid=9):
    def kernel(x_ref, o_ref, got, send, recv):
        me = lax.axis_index("dp")
        sem = pltpu.get_barrier_semaphore()
        def other(k):
            return lax.rem(me + k, n)
        def greet(k, _):
            pl.semaphore_signal(sem, inc=1, device_id={"dp": other(k)}, device_id_type=MESH)
            return 0
        lax.fori_loop(1, n, greet, 0)
        pl.semaphore_wait(sem, n - 1)
        def copy(k, slot):
            return pltpu.make_async_remote_copy(src_ref=x_ref, dst_ref=got.at[slot], send_sem=send.at[k], recv_sem=recv.at[slot], device_id={"dp": other(k)}, device_id_type=MESH)
        def start(k, _):
            copy(k, me).start()
            return 0
        lax.fori_loop(1, n, start, 0)
        got[me] = x_ref[...]
        def wait(k, _):
            copy(k, me).wait_send()
            copy(k, other(k)).wait_recv()
            return 0
        lax.fori_loop(1, n, wait, 0)
        o_ref[...] = jnp.sum(got[...], axis=0)
    V = pl.BlockSpec(memory_space=pltpu.VMEM)
    D = pltpu.SemaphoreType.DMA
    return pl.pallas_call(
        kernel, name="total", out_shape=jax.ShapeDtypeStruct(part.shape, jnp.float32), in_specs=[V], out_specs=V,
        scratch_shapes=[pltpu.VMEM((n, *part.shape), jnp.float32), D((n,)), D((n,))],
        compiler_params=pltpu.CompilerParams(collective_id=cid, has_side_effects=True),
    )(part)


def adamw(w, m, v, g):
    m = 0.9 * m + 0.1 * g
    v = 0.95 * v + 0.05 * g * g
    step = m * lax.rsqrt(v + 1e-8) + 0.1 * w
    return (w - 0.02 * step).astype(bf), m, v


def solution(mesh):
    n = mesh.shape["dp"]

    def step(x, dy, *arrays):
        weights, m, v = (arrays[i : i + 3] for i in (0, 3, 6))
        x, dy = x[0], dy[0]
        wgu, wd, g0, u0, act0, h1, a0, a1, act1, dg1, du1 = forward(n, x, dy, *weights, lag=2)
        *mine1, sq1, dh1 = backward_last(n, a1, act1, dg1, du1, dy, h1, wgu, 1)
        *mine0, sq0 = backward_first(n, a0, act0, g0, u0, dh1, wd, 0)
        squares = jnp.sum(total(n, sq0 + sq1))
        count = n * sum(w.size for w in weights)
        factor = jnp.minimum(1.0, 0.5 * lax.rsqrt(squares / count + 1e-30))
        gradients = [jnp.stack(g).astype(f32) * factor for g in zip(mine0, mine1, strict=True)]
        new = [adamw(w.astype(f32), m, v, g) for w, m, v, g in zip(weights, m, v, gradients, strict=True)]
        return tuple(one[which] for which in range(3) for one in new)

    states, cut = P(("rep", "dp"), None, None), P(None, "dp", None)
    return jax.shard_map(
        step,
        mesh=mesh,
        in_specs=(states, states) + (cut,) * 9,
        out_specs=(P("rep", "dp", None),) * 9,
        check_vma=False,
    )
```

time: 930 us -> 374 us (0.40)
  waiting for transfers between devices: 486 us -> 0 us
  Pallas kernels: 0 us -> 362 us
  matrix products: 331 us -> 0 us
  blocking collectives: 46.3 us -> 0 us
  local copies, waits for them, and re-layouts: 20.4 us -> 0 us
  between operations: 17.5 us -> 1.37 us
    pallas_call x0 -> x4, Pallas kernels: none -> 362 us  [the longest x1 140 us: forward(): pl.pallas_call(kernel, name='forward', out_shape=[S((L, side, side, 2, 2,...]
    reduce_scatter x6 -> x0, waiting for transfers between devices: 341 us -> none  [step(): lax.psum_scatter(by_w[name], 'dp', scatter_dimension=0, tiled=True)]
    dot_general x15 -> x0, matrix products: 331 us -> none  [the longest x5 119 us: layer(): gate = jnp.dot(a, w['w_gate'], preferred_element_type=jnp.float32)]
    all_gather x6 -> x0, waiting for transfers between devices: 143 us -> none  [fetched(): lax.all_gather(w[number], 'dp', axis=0, tiled=True)]
    psum x1 -> x0, blocking collectives: 46.3 us -> none  [step(): squares = lax.psum(sum((jnp.sum(g * g) for g in gradients)), 'dp')]
    unnamed x32 -> x0, local copies, waits for them, and re-layouts: 15.1 us -> none
  transfers between devices with their start and end apart: 12 -> 0, of which waited for: 11 -> 0; matrix products, arithmetic and copies ran while one was open for 29% -> 0% of each run, Pallas kernels for 0% -> 0%
where the time goes in v2:
time: 374 us; the launch traced here: 373 us
  Pallas kernels  362 us (97%)
  other arithmetic  9.99 us (3%)
    pallas_call x1, Pallas kernels, forward(): pl.pallas_call(kernel, name='forward', out_shape=[S((L, side, side, 2, 2,...  140 us
    pallas_call x1, Pallas kernels, backward_last(): pl.pallas_call(kernel, name='backward_last', out_shape=[*k.outs(), jax.Sh...  105 us
    pallas_call x1, Pallas kernels, backward_first(): pl.pallas_call(kernel, name='backward_first', out_shape=k.outs(), in_spec...  102 us
    pallas_call x1, Pallas kernels, total(): pl.pallas_call(kernel, name='total', out_shape=jax.ShapeDtypeStruct(part....  14.4 us

profile of v2, /device:TPU:97, one launch (start us, length us, event | category | flops | bytes accessed | tf_op | source)
XLA Modules:
  0.0 373.3 jit_solution(5344671476351454532)
XLA Ops:
  0.6 140.1 %forward.1 = (bf16[2,4,4,2,2,32,2816]{6,5,4,3,2,1,0:T(8,128)(2,1)}, bf16[2,4,4,176,1024]{4,3,2,1,0:T(8,128)(2,1)}, f32[2048,2816]{1,0:T(8,128)}, f32[2048,2816]{...) custom-call(bf16[2048,1024]{1,0:T(8,128)(2,1)} %bitcast.12, ...), custom_call_target="tpu_custom_call" | custom-call | tf_op jit(solution)/shard_map/forward/pallas_call | solution.py:418
  140.7 105.3 %backward_last.1 = (bf16[32,2816]{1,0:T(8,128)(2,1)}, bf16[32,2816]{1,0:T(8,128)(2,1)}, bf16[88,1024]{1,0:T(8,128)(2,1)}, f32[8,128]{1,0:T(8,128)}, bf16[2048,1024]{1,0:T(8,128)(2,1)}) custom-call(bf16[2048,1024]{1,0:T(8,128)(2,1)} %get-tuple-element.33.a_h, bf16[2048,2816]{1,0:T(8,128)(2,1)} %get-tuple-element.34.act_h, ...), custom_call_target="tpu_custom_call" | custom-call | tf_op jit(solution)/shard_map/backward_last/pallas_call | solution.py:588
  246.0 102.2 %backward_first.1 = (bf16[32,2816]{1,0:T(8,128)(2,1)}, bf16[32,2816]{1,0:T(8,128)(2,1)}, bf16[88,1024]{1,0:T(8,128)(2,1)}, f32[8,128]{1,0:T(8,128)}) custom-call(bf16[2048,1024]{1,0:T(8,128)(2,1)} %get-tuple-element.29.a_h, bf16[2048,2816]{1,0:T(8,128)(2,1)} %get-tuple-element.30.act_h, f32[2048,2816]{1,0:T(8,128)} %get-tuple-element.31.g_h, ...), custom_call_target="tpu_custom_call" | custom-call | tf_op jit(solution)/shard_map/backward_first/pallas_call | solution.py:655
  348.3 1.3 add.45.x_ref
  349.6 14.4 %total.1 = f32[8,128]{1,0:T(8,128)} custom-call(f32[8,128]{1,0:T(8,128)} %add.45.x_ref), custom_call_target="tpu_custom_call" | custom-call | tf_op jit(solution)/shard_map/total/pallas_call | solution.py:689
  363.9 1.3 reduce_sum.9
  365.9 3.0 fusion.8
  368.9 4.4 %fusion.2 = (bf16[2,32,2816]{2,1,0:T(8,128)(2,1)}, f32[2,32,2816]{2,1,0:T(8,128)}, f32[2,32,2816]{2,1,0:T(8,128)}, bf16[2,32,2816]{2,1,0:T(8,128)(2,1)}, f32[2,32,2816]{2,1,0:T(8,128)}, /*index=5*/f32[2,32,2816]{2,1,0:T(8,128)}) fusion(bf16[2,32,2816]{2,1,0:T(8,128)(2,1)} %wg_ref.1, f32[]{:T(128)S(6)} %min_shard_map.3, bf16[1,32,2816]{2,1,0:T(8,128)(2,1)} %bitcast.15, ...), kind=kLoop, calls=%fused_computation.11 | loop fusion | flops 7208960 | bytes 7929860 | tf_op jit(solution)/shard_map/convert_element_type | solution.py:700

commit v3 on v2

--- a/solution.py
+++ b/solution.py
@@ -185,14 +185,14 @@
 
 
 def scatter_slots(m, lag):
-    return min(m, 3 * lag), min(m, lag + 1)
+    return min(m, 3 * lag), min(m, lag)
 
 
 def scatter_bufs(m, lag, side, R, C):
     keep, pool = scatter_slots(m, lag)
-    few, V, D = min(m, lag + 1), pltpu.VMEM, pltpu.SemaphoreType.DMA
+    few, V, D = min(m, lag), pltpu.VMEM, pltpu.SemaphoreType.DMA
     pairs = [V((k, 2, *s, R, C), bf) for s in ((2, side), (side,), (2,), ()) for k in (few, m)]
-    return [V((keep + pool, 2, side * side, R, C), bf), V((m, 2, side * side, R, C), bf), V((min(m, 2 * lag + 1), 2, side, R, C), f32), *pairs,
+    return [V((keep + pool, 2, side * side, R, C), bf), V((m, 2, side * side, R, C), bf), V((min(m, 2 * lag), 2, side, R, C), f32), *pairs,
             D((m,)), D((m,)), D((m, 4, 2)), D((m, 4, 2))]
 
 
@@ -202,7 +202,7 @@
     return (wide * scale).astype(bf)
 
 
-def forward(n, x, dy, wg, wu, wd, lag=3, cg=256, cd=128, cid=1):
+def forward(n, x, dy, wg, wu, wd, lag=2, cg=256, cd=128, cid=1):
     side = math.isqrt(n // 2)
     T, Dm = x.shape
     L, R, F = wg.shape
@@ -210,7 +210,7 @@
     ng, nd, rows, tile = F // cg, Dm // (2 * cd), T // 2, T // 8
     width = 2 * cd
 
-    def kernel(x_h, dy_h, wg_ref, wu_ref, wd_ref, ogu, od, g0, u0, act0, h1, a0, a1, act1, dg1, du1,
+    def kernel(x_h, dy_h, wg_ref, wu_ref, wd_ref, ogu, od, g0, u0, act0, h1, a0, a1, act1, dgu1,
                xv, av, dyv, actv, own_v, wb, wdb, wdr, stg, st3, s_in, s_w, s_wd, s_wr, s_stg, s_act, s_out, s_st3, *sems):
         p = Place(n)
         pltpu.make_async_copy(x_h, xv, s_in.at[0]).start()
@@ -276,7 +276,8 @@
         def put_act(j):
             return pltpu.make_async_copy(actv.at[:, cols(j, cg)], act0.at[:, cols(j, cg)], s_act.at[j])
         def put_3(j, r):
-            return [pltpu.make_async_copy(st3.at[r, e], (act1, dg1, du1)[e].at[part(r), cols(j, cg)], s_st3.at[r, e]) for e in (0, 1, 2)]
+            to = [act1.at[part(r), cols(j, cg)], *(dgu1.at[e, part(r), cols(j, cg)] for e in BOTH)]
+            return [pltpu.make_async_copy(st3.at[r, e], ref, s_st3.at[r, e]) for e, ref in enumerate(to)]
         put_a0 = pltpu.make_async_copy(av, a0, s_out.at[0])
         put_h1 = pltpu.make_async_copy(xv, h1, s_out.at[1])
         put_a1 = pltpu.make_async_copy(av, a1, s_out.at[2])
@@ -304,9 +305,11 @@
                 a = av[part(r), :]
                 g = jnp.dot(a, weights(j, 0), preferred_element_type=f32)
                 u = jnp.dot(a, weights(j, 1), preferred_element_type=f32)
-                stg[r, 0] = g
-                stg[r, 1] = u
-                actv[part(r), cols(j, cg)] = (g * jax.nn.sigmoid(g) * u).astype(bf)
+                s = jax.nn.sigmoid(g)
+                gs = g * s
+                stg[r, 0] = u * (s + gs * (1.0 - s))
+                stg[r, 1] = gs
+                actv[part(r), cols(j, cg)] = (gs * u).astype(bf)
                 for c in put_g(j, r):
                     c.start()
                 return 0
@@ -418,8 +421,8 @@
     out = pl.pallas_call(
         kernel, name="forward",
         out_shape=[S((L, side, side, 2, 2, R, F), bf), S((L, side, side, 2 * Rd, Dm), bf),
-                   S((T, F), f32), S((T, F), f32), wide, thin, thin, thin, wide, wide, wide],
-        in_specs=[A, A, V, V, V], out_specs=[A] * 11,
+                   S((T, F), f32), S((T, F), f32), wide, thin, thin, thin, wide, S((2, T, F), bf)],
+        in_specs=[A, A, V, V, V], out_specs=[A] * 10,
         scratch_shapes=[VM((T, Dm), bf), VM((T, Dm), bf), VM((T, Dm), bf), VM((T, F), bf), VM((L, 2, R, F), bf), VM((2, side, side, 2, 2, R, cg), bf), VM((2, side, side, 2 * Rd, width), bf), VM((F, Dm), bf),
                         VM((2, 2, rows, cg), f32), VM((2, 3, rows, cg), bf),
                         D((2,)), D((2,)), D((2,)), D((side * side,)), D((2, 2)), D((ng,)), D((3,)), D((2, 3)), *sems],
@@ -427,6 +430,63 @@
     )(x, dy, wg, wu, wd)
     ogu, od, *rest = out
     return ogu, od.reshape(L, n * Rd, Dm), *rest
+
+
+def greet_all(n):
+    me, sem = lax.axis_index("dp"), pltpu.get_barrier_semaphore()
+    def greet(k, _):
+        pl.semaphore_signal(sem, inc=1, device_id={"dp": lax.rem(me + k, n)}, device_id_type=MESH)
+        return 0
+    lax.fori_loop(1, n, greet, 0)
+    pl.semaphore_wait(sem, n - 1)
+
+
+def clip(n, count, part, o_ref, x_ref, got, send, recv):
+    me = lax.axis_index("dp")
+    x_ref[...] = part
+    def copy(k, slot):
+        return pltpu.make_async_remote_copy(src_ref=x_ref, dst_ref=got.at[slot], send_sem=send.at[k], recv_sem=recv.at[slot], device_id={"dp": lax.rem(me + k, n)}, device_id_type=MESH)
+    def start(k, _):
+        copy(k, me).start()
+        return 0
+    lax.fori_loop(1, n, start, 0)
+    got[me] = part
+    def wait(k, _):
+        copy(k, me).wait_send()
+        copy(k, lax.rem(me + k, n)).wait_recv()
+        return 0
+    lax.fori_loop(1, n, wait, 0)
+    o_ref[...] = jnp.minimum(1.0, 0.5 * lax.rsqrt(jnp.full_like(part, jnp.sum(got[...])) / count + 1e-30))
+
+
+def update(factor, weights, moments, squares, grads):
+    L = len(grads)
+    def kernel(f_ref, *refs):
+        f, layer = f_ref[0, 0], pl.program_id(0)
+        ins, outs = refs[:-9], refs[-9:]
+        for i in range(3):
+            w, m, v = (ins[3 * k + i][0].astype(jnp.float32) for k in range(3))
+            g = ins[9 + i][...].astype(jnp.float32)
+            for l in range(1, L):
+                g = jnp.where(layer == l, ins[9 + 3 * l + i][...].astype(jnp.float32), g)
+            g = g * f
+            m = 0.9 * m + 0.1 * g
+            v = 0.95 * v + 0.05 * g * g
+            step = m * lax.rsqrt(v + 1e-8) + 0.1 * w
+            outs[i][0] = (w - 0.02 * step).astype(bf)
+            outs[3 + i][0] = m
+            outs[6 + i][0] = v
+    def whole(a):
+        return pl.BlockSpec((1, a.shape[1], a.shape[2] // 2), lambda l, c: (l, 0, c))
+    arrays = (*weights, *moments, *squares)
+    flat = [g for layer in grads for g in layer]
+    S = jax.ShapeDtypeStruct
+    return pl.pallas_call(
+        kernel, name="update", grid=(L, 2),
+        out_shape=[S(a.shape, a.dtype) for a in arrays],
+        in_specs=[pl.BlockSpec(memory_space=pltpu.SMEM), *map(whole, arrays), *(pl.BlockSpec((g.shape[0], g.shape[1] // 2), lambda l, c: (0, c)) for g in flat)],
+        out_specs=[*map(whole, arrays)],
+    )(factor, *arrays, *flat)
 
 
 class Layer:
@@ -490,15 +550,19 @@
         lax.fori_loop(0, total, body, 0)
 
 
+def tall_product(ref, lo, hi, rhs, most=768):
+    return jnp.concatenate([lax.dot_general(ref[:rhs.shape[0], m:min(m + most, hi)], rhs, TN, preferred_element_type=f32) for m in range(lo, hi, most)], 0)
+
+
 def cols_of(j, w):
     return pl.ds(pl.multiple_of(j * w, w), w)
 
 
-def backward_last(n, a, act, dgate, dup, dy, h, wgu, layer, lag=2, lagd=2, cg=256, cd=128, cid=2):
+def backward_last(n, a, act, dgu, dy, h, wgu, layer, lag=2, lagd=2, cg=256, cd=128, cid=2):
     k = Layer(n, a, act, lag, lagd, cg, cd)
-    T, Dm, F, tile = k.T, k.Dm, k.F, k.T // 8
-    def kernel(a_h, act_h, dg_h, du_h, dy_h, h_h, w_h, og, ou, od, sq, dh_h,
-               a_v, act_v, dg_v, dy_v, row_v, h_v, y_v, o_v, ld, ldg, ldy, ldr, ldo, ldw, *bufs):
+    T, Dm, F, tile = k.T, k.Dm, k.F, k.T // k.nd
+    def kernel(a_h, act_h, dgu_h, dy_h, h_h, w_h, og, ou, od, sq, dh_h,
+               a_v, act_v, dg_v, dy_v, row_v, part_v, ld, ldg, ldy, ldr, ldo, ldw, *bufs):
         p = Place(n)
         def load_act(m):
             cols = pl.ds(m * k.half, k.half)
@@ -507,7 +571,7 @@
         def load_dy(j):
             return pltpu.make_async_copy(dy_h.at[:, cols_of(j, 2 * cd)], dy_v.at[lax.rem(j, 2)], ldy.at[lax.rem(j, 2)])
         def load_dg(j, e):
-            return pltpu.make_async_copy((dg_h, du_h)[e].at[:, cols_of(j, cg)], dg_v.at[lax.rem(j, 2), :, e * cg:(e + 1) * cg], ldg.at[lax.rem(j, 2), e])
+            return pltpu.make_async_copy(dgu_h.at[e, :, cols_of(j, cg)], dg_v.at[lax.rem(j, 2), :, e * cg:(e + 1) * cg], ldg.at[lax.rem(j, 2), e])
         def load_w(d):
             for e in BOTH:
                 chip = d // 2
@@ -516,13 +580,25 @@
             return 0
         w_v = act_v.at[:2 * Dm]
         def load_row(r, e):
-            return pltpu.make_async_copy((dg_h, du_h)[e].at[cols_of(r, tile), :], row_v.at[e], ldr.at[e])
+            return pltpu.make_async_copy(dgu_h.at[e, cols_of(r, tile), :], row_v.at[e], ldr.at[e])
+        def blocks(ref, r, v):
+            return [(ref.at[cols_of(r, tile), c * 2 * cd:(c + 1) * 2 * cd], v.at[c * tile:(c + 1) * tile]) for c in range(k.nd)]
+        h_v, y_v = dy_v.at[0], dy_v.at[1]
+        def load_tile(ref, r, v, sem):
+            for src, dst in blocks(ref, r, v):
+                pltpu.make_async_copy(src, dst, sem).start()
         def load_h(r):
-            return pltpu.make_async_copy(h_h.at[cols_of(r, tile), :], h_v, ldr.at[2])
+            load_tile(h_h, r, h_v, ldr.at[2])
         def load_y(r):
-            return pltpu.make_async_copy(dy_h.at[cols_of(r, tile), :], y_v, ldr.at[3])
+            load_tile(dy_h, r, y_v, ldr.at[3])
         def put(r):
-            return pltpu.make_async_copy(o_v, dh_h.at[cols_of(r, tile), :], ldo)
+            for dst, src in blocks(dh_h, r, y_v):
+                pltpu.make_async_copy(src, dst, ldo).start()
+        def arrived(v, sem):
+            pltpu.make_async_copy(v, v, sem).wait()
+        def tile_of(v, m):
+            return jnp.concatenate([v[pl.ds(pl.multiple_of(c * tile + m * part, part), part)] for c in range(k.nd)], 1)
+        part = tile // 4
         load_dy(0).start(); load_act(0).start(); load_act(1).start()
         barrier(p)
         k.streams(p, og, ou, od, sq, bufs)
@@ -539,7 +615,7 @@
                 if m == 1:
                     @pl.when(j == 0)
                     def _(): load_act(1).wait()
-                k.put_d(j, m, lax.dot_general(act_v[:T, m * k.half:(m + 1) * k.half], dy_v[lax.rem(j, 2)], TN, preferred_element_type=f32))
+                k.put_d(j, m, tall_product(act_v, m * k.half, (m + 1) * k.half, dy_v[lax.rem(j, 2)]))
             k.sd.send(j)
             @pl.when(j + 1 < k.nd)
             def _(): load_dy(j + 1).wait()
@@ -554,49 +630,60 @@
             @pl.when(j == k.ng - 1)
             def _():
                 for e in BOTH: load_row(0, e).start()
-                load_h(0).start(); load_y(0).start()
+                load_h(0)
+                load_y(0)
             for e in BOTH:
                 load_dg(j, e).wait()
             k.put_g(j, lax.dot_general(a_v[...], dg_v[lax.rem(j, 2)], TN, preferred_element_type=f32))
             k.sg.send(j)
-        def rows(r):
-            @pl.when(r == 0)
+        def rows(i):
+            r, e = i // 2, lax.rem(i, 2)
+            @pl.when(i == 0)
             def _():
                 pltpu.make_async_copy(w_v, w_v, ldw).wait()
-            @pl.when(r > 0)
-            def _():
-                put(r - 1).wait()
-            def again(c):
+            @pl.when((e == 0) & (r > 0))
+            def _():
+                arrived(y_v, ldo)
+                load_y(r)
+            load_row(r, e).wait()
+            part_v[e] = lax.dot_general(row_v[e], act_v[pl.ds(pl.multiple_of(e * Dm, Dm), Dm)], NT, preferred_element_type=f32).astype(bf)
+            @pl.when(r + 1 < T // tile)
+            def _():
+                load_row(r + 1, e).start()
+            @pl.when(e == 1)
+            def _():
+                arrived(h_v, ldr.at[2])
+                arrived(y_v, ldr.at[3])
+                def one(m, _):
+                    some = cols_of(m, part)
+                    da = (part_v[0, some] + part_v[1, some]).astype(f32)
+                    wide = tile_of(h_v, m).astype(f32)
+                    s = lax.rsqrt(jnp.mean(wide * wide, -1, keepdims=True) + 1e-6)
+                    t = jnp.sum(da * wide, -1, keepdims=True) * (s * s * s) * (1.0 / Dm)
+                    new = (da * s - wide * t).astype(bf) + tile_of(y_v, m)
+                    for c in range(k.nd):
+                        y_v[pl.ds(pl.multiple_of(c * tile + m * part, part), part)] = new[:, c * 2 * cd:(c + 1) * 2 * cd]
+                    return 0
+                lax.fori_loop(0, 4, one, 0)
+                put(r)
                 @pl.when(r + 1 < T // tile)
-                def _(): c.start()
-            both = []
-            for e in BOTH:
-                load_row(r, e).wait()
-                both.append(lax.dot_general(row_v[e], act_v[e * Dm:(e + 1) * Dm], NT, preferred_element_type=f32).astype(bf))
-                again(load_row(r + 1, e))
-            da = (both[0] + both[1]).astype(f32)
-            load_h(r).wait(); load_y(r).wait()
-            wide = h_v[...].astype(f32)
-            s = lax.rsqrt(jnp.mean(wide * wide, -1, keepdims=True) + 1e-6)
-            t = jnp.sum(da * wide, -1, keepdims=True) * (s * s * s) * (1.0 / Dm)
-            o_v[...] = (da * s - wide * t).astype(bf) + y_v[...]
-            put(r).start()
-            again(load_h(r + 1)); again(load_y(r + 1))
-        k.run(make_d, make_g, T // tile, rows)
-        put(T // tile - 1).wait()
+                def _():
+                    load_h(r + 1)
+        k.run(make_d, make_g, 2 * (T // tile), rows)
+        arrived(y_v, ldo)
     V, A, D, VM = pl.BlockSpec(memory_space=pltpu.VMEM), pl.BlockSpec(memory_space=pl.ANY), pltpu.SemaphoreType.DMA, pltpu.VMEM
     return pl.pallas_call(
-        kernel, name="backward_last", out_shape=[*k.outs(), jax.ShapeDtypeStruct((T, Dm), bf)], in_specs=[A] * 7, out_specs=[V] * 4 + [A],
-        scratch_shapes=[VM((T, Dm), bf), VM((max(T, 2 * Dm), F), bf), VM((2, T, 2 * cg), bf), VM((2, T, 2 * cd), bf), VM((2, tile, F), bf), VM((tile, Dm), bf), VM((tile, Dm), bf), VM((tile, Dm), bf),
+        kernel, name="backward_last", out_shape=[*k.outs(), jax.ShapeDtypeStruct((T, Dm), bf)], in_specs=[A] * 6, out_specs=[V] * 4 + [A],
+        scratch_shapes=[VM((T, Dm), bf), VM((max(T, 2 * Dm), F), bf), VM((2, T, 2 * cg), bf), VM((2, T, 2 * cd), bf), VM((2, tile, F), bf), VM((2, tile, Dm), bf),
                         D((3,)), D((2, 2)), D((2,)), D((4,)), D, D, *k.bufs()],
         compiler_params=pltpu.CompilerParams(collective_id=cid, has_side_effects=True, vmem_limit_bytes=67043328),
-    )(a, act, dgate, dup, dy, h, wgu)
-
-
-def backward_first(n, a, act, gate, up, dh, wd, layer, lag=2, lagd=2, cg=256, cd=128, cid=3):
+    )(a, act, dgu, dy, h, wgu)
+
+
+def backward_first(n, a, act, by_gate, by_up, dh, wd, sq_last, count, layer, lag=2, lagd=2, cg=256, cd=128, cid=3):
     k = Layer(n, a, act, lag, lagd, cg, cd)
     T, Dm, F, rows = k.T, k.Dm, k.F, k.T // 2
-    def kernel(a_h, act_h, g_h, u_h, dh_h, wd_h, og, ou, od, sq, a_v, act_v, gu_v, dg_v, dh_v, wd_v, ld, ldg, ldw, *bufs):
+    def kernel(a_h, act_h, g_h, u_h, dh_h, wd_h, sq_ref, og, ou, od, factor, a_v, act_v, gu_v, dg_v, dh_v, wd_v, ld, ldg, ldw, sq, part_v, got, send, recv, *bufs):
         p = Place(n)
         def load_act(m):
             cols = pl.ds(m * k.half, k.half)
@@ -610,7 +697,7 @@
         def load_wd(j):
             return pltpu.make_async_copy(wd_h.at[layer, cols_of(j, cg), :], wd_v, ldw)
         load_dh.start(); load_act(0).start(); load_act(1).start()
-        barrier(p)
+        greet_all(n)
         k.streams(p, og, ou, od, sq, bufs)
         load_dh.wait(); load_act(0).wait()
         def make_d(j):
@@ -625,7 +712,7 @@
                 if m == 1:
                     @pl.when(j == 0)
                     def _(): load_act(1).wait()
-                k.put_d(j, m, lax.dot_general(act_v[:, m * k.half:(m + 1) * k.half], dh_v[:, cols_of(j, 2 * cd)], TN, preferred_element_type=f32))
+                k.put_d(j, m, tall_product(act_v, m * k.half, (m + 1) * k.half, dh_v[:, cols_of(j, 2 * cd)]))
             k.sd.send(j)
         def make_g(j):
             @pl.when(j == 0)
@@ -635,11 +722,8 @@
                 for c in load_gu(j, r):
                     c.wait()
                 d = lax.dot_general(dh_v[part(r), :], wd_v[...], NT, preferred_element_type=f32).astype(bf).astype(f32)
-                g, u = gu_v[r, 0], gu_v[r, 1]
-                s = jax.nn.sigmoid(g)
-                gs = g * s
-                dg_v[part(r), :cg] = (d * u * (s + gs * (1.0 - s))).astype(bf)
-                dg_v[part(r), cg:] = (d * gs).astype(bf)
+                for e in BOTH:
+                    dg_v[part(r), e * cg:(e + 1) * cg] = (d * gu_v[r, e]).astype(bf)
                 @pl.when(j + 1 < k.ng)
                 def _():
                     for c in load_gu(j + 1, r): c.start()
@@ -651,53 +735,14 @@
             k.put_g(j, lax.dot_general(a_v[...], dg_v[...], TN, preferred_element_type=f32))
             k.sg.send(j)
         k.run(make_d, make_g)
+        clip(n, count, sq[...] + sq_ref[...], factor, part_v, got, send, recv)
     V, A, D, VM = pl.BlockSpec(memory_space=pltpu.VMEM), pl.BlockSpec(memory_space=pl.ANY), pltpu.SemaphoreType.DMA, pltpu.VMEM
     return pl.pallas_call(
-        kernel, name="backward_first", out_shape=k.outs(), in_specs=[A] * 6, out_specs=[V] * 4,
+        kernel, name="backward_first", out_shape=k.outs(), in_specs=[A] * 6 + [V], out_specs=[V] * 4,
         scratch_shapes=[VM((T, Dm), bf), VM((T, F), bf), VM((2, 2, rows, cg), f32), VM((T, 2 * cg), bf), VM((T, Dm), bf), VM((cg, Dm), bf),
-                        D((4,)), D((2, 2)), D, *k.bufs()],
+                        D((4,)), D((2, 2)), D, VM((8, 128), f32), VM((8, 128), f32), VM((n, 8, 128), f32), D((n,)), D((n,)), *k.bufs()],
         compiler_params=pltpu.CompilerParams(collective_id=cid, has_side_effects=True, vmem_limit_bytes=67043328),
-    )(a, act, gate, up, dh, wd)
-
-
-def total(n, part, cid=9):
-    def kernel(x_ref, o_ref, got, send, recv):
-        me = lax.axis_index("dp")
-        sem = pltpu.get_barrier_semaphore()
-        def other(k):
-            return lax.rem(me + k, n)
-        def greet(k, _):
-            pl.semaphore_signal(sem, inc=1, device_id={"dp": other(k)}, device_id_type=MESH)
-            return 0
-        lax.fori_loop(1, n, greet, 0)
-        pl.semaphore_wait(sem, n - 1)
-        def copy(k, slot):
-            return pltpu.make_async_remote_copy(src_ref=x_ref, dst_ref=got.at[slot], send_sem=send.at[k], recv_sem=recv.at[slot], device_id={"dp": other(k)}, device_id_type=MESH)
-        def start(k, _):
-            copy(k, me).start()
-            return 0
-        lax.fori_loop(1, n, start, 0)
-        got[me] = x_ref[...]
-        def wait(k, _):
-            copy(k, me).wait_send()
-            copy(k, other(k)).wait_recv()
-            return 0
-        lax.fori_loop(1, n, wait, 0)
-        o_ref[...] = jnp.sum(got[...], axis=0)
-    V = pl.BlockSpec(memory_space=pltpu.VMEM)
-    D = pltpu.SemaphoreType.DMA
-    return pl.pallas_call(
-        kernel, name="total", out_shape=jax.ShapeDtypeStruct(part.shape, jnp.float32), in_specs=[V], out_specs=V,
-        scratch_shapes=[pltpu.VMEM((n, *part.shape), jnp.float32), D((n,)), D((n,))],
-        compiler_params=pltpu.CompilerParams(collective_id=cid, has_side_effects=True),
-    )(part)
-
-
-def adamw(w, m, v, g):
-    m = 0.9 * m + 0.1 * g
-    v = 0.95 * v + 0.05 * g * g
-    step = m * lax.rsqrt(v + 1e-8) + 0.1 * w
-    return (w - 0.02 * step).astype(bf), m, v
+    )(a, act, by_gate, by_up, dh, wd, sq_last)
 
 
 def solution(mesh):
@@ -706,15 +751,10 @@
     def step(x, dy, *arrays):
         weights, m, v = (arrays[i : i + 3] for i in (0, 3, 6))
         x, dy = x[0], dy[0]
-        wgu, wd, g0, u0, act0, h1, a0, a1, act1, dg1, du1 = forward(n, x, dy, *weights, lag=2)
-        *mine1, sq1, dh1 = backward_last(n, a1, act1, dg1, du1, dy, h1, wgu, 1)
-        *mine0, sq0 = backward_first(n, a0, act0, g0, u0, dh1, wd, 0)
-        squares = jnp.sum(total(n, sq0 + sq1))
-        count = n * sum(w.size for w in weights)
-        factor = jnp.minimum(1.0, 0.5 * lax.rsqrt(squares / count + 1e-30))
-        gradients = [jnp.stack(g).astype(f32) * factor for g in zip(mine0, mine1, strict=True)]
-        new = [adamw(w.astype(f32), m, v, g) for w, m, v, g in zip(weights, m, v, gradients, strict=True)]
-        return tuple(one[which] for which in range(3) for one in new)
+        wgu, wd, g0, u0, act0, h1, a0, a1, act1, dgu1 = forward(n, x, dy, *weights)
+        *mine1, sq1, dh1 = backward_last(n, a1, act1, dgu1, dy, h1, wgu, 1)
+        *mine0, factor = backward_first(n, a0, act0, g0, u0, dh1, wd, sq1, n * sum(w.size for w in weights), 0)
+        return tuple(update(factor, weights, m, v, (mine0, mine1)))
 
     states, cut = P(("rep", "dp"), None, None), P(None, "dp", None)
     return jax.shard_map(

time: 374 us -> 339 us (0.906)
  Pallas kernels: 362 us -> 337 us
  other arithmetic: 9.99 us -> 0 us
    pallas_call x1, Pallas kernels: 105 us -> 92.4 us  [backward_last(): pl.pallas_call(kernel, name='backward_last', out_shape=[*k.outs(), jax.Sh...]
    pallas_call x1, Pallas kernels: 14.4 us -> 6.19 us  [update(): pl.pallas_call(kernel, name='update', grid=(L, 2), out_shape=[S(a.shape,...]
    convert_element_type x2 -> x0, other arithmetic: 7.42 us -> none  [adamw(): return ((w - 0.02 * step).astype(bf), m, v)]
    pallas_call x1, Pallas kernels: 102 us -> 98.4 us  [backward_first(): pl.pallas_call(kernel, name='backward_first', out_shape=k.outs(), in_spec...]
where the time goes in v3:
time: 339 us; the launch traced here: 338 us
  Pallas kernels  337 us (99%)
    pallas_call x1, Pallas kernels, forward(): pl.pallas_call(kernel, name='forward', out_shape=[S((L, side, side, 2, 2,...  140 us
    pallas_call x1, Pallas kernels, backward_first(): pl.pallas_call(kernel, name='backward_first', out_shape=k.outs(), in_spec...  98.4 us
    pallas_call x1, Pallas kernels, backward_last(): pl.pallas_call(kernel, name='backward_last', out_shape=[*k.outs(), jax.Sh...  92.4 us

profile of v3, /device:TPU:97, one launch (start us, length us, event | category | flops | bytes accessed | tf_op | source)
XLA Modules:
  0.0 338.3 jit_solution(7068868364497432545)
XLA Ops:
  0.6 140.4 %forward.1 = (bf16[2,4,4,2,2,32,2816]{6,5,4,3,2,1,0:T(8,128)(2,1)}, bf16[2,4,4,176,1024]{4,3,2,1,0:T(8,128)(2,1)}, f32[2048,2816]{1,0:T(8,128)}, f32[2048,2816]{...) custom-call(bf16[2048,1024]{1,0:T(8,128)(2,1)} %bitcast.6, ...), custom_call_target="tpu_custom_call" | custom-call | tf_op jit(solution)/shard_map/forward/pallas_call | solution.py:421
  141.1 92.4 %backward_last.1 = (bf16[32,2816]{1,0:T(8,128)(2,1)}, bf16[32,2816]{1,0:T(8,128)(2,1)}, bf16[88,1024]{1,0:T(8,128)(2,1)}, f32[8,128]{1,0:T(8,128)}, bf16[2048,1024]{1,0:T(8,128)(2,1)}) custom-call(bf16[2048,1024]{1,0:T(8,128)(2,1)} %get-tuple-element.32.a_h, bf16[2048,2816]{1,0:T(8,128)(2,1)} %get-tuple-element.33.act_h, ...), custom_call_target="tpu_custom_call" | custom-call | tf_op jit(solution)/shard_map/backward_last/pallas_call | solution.py:675
  233.5 98.4 %backward_first.1 = (bf16[32,2816]{1,0:T(8,128)(2,1)}, bf16[32,2816]{1,0:T(8,128)(2,1)}, bf16[88,1024]{1,0:T(8,128)(2,1)}, f32[8,128]{1,0:T(8,128)}) custom-call(bf16[2048,1024]{1,0:T(8,128)(2,1)} %get-tuple-element.28.a_h, bf16[2048,2816]{1,0:T(8,128)(2,1)} %get-tuple-element.29.act_h, f32[2048,2816]{1,0:T(8,128)} %get-tuple-element.30.g_h, ...), custom_call_target="tpu_custom_call" | custom-call | tf_op jit(solution)/shard_map/backward_first/pallas_call | solution.py:740
  331.9 6.2 %update.1 = (bf16[2,32,2816]{2,1,0:T(8,128)(2,1)}, bf16[2,32,2816]{2,1,0:T(8,128)(2,1)}, bf16[2,88,1024]{2,1,0:T(8,128)(2,1)}, f32[2,32,2816]{2,1,0:T(8,128)}, f...) custom-call(f32[8,128]{1,0:T(8,128)} %get-tuple-element.40.f_ref, ...), custom_call_target="tpu_custom_call" | custom-call | tf_op jit(solution)/shard_map/update/pallas_call | solution.py:484

commit v4 on v3

--- a/solution.py
+++ b/solution.py
@@ -550,8 +550,22 @@
         lax.fori_loop(0, total, body, 0)
 
 
-def tall_product(ref, lo, hi, rhs, most=768):
-    return jnp.concatenate([lax.dot_general(ref[:rhs.shape[0], m:min(m + most, hi)], rhs, TN, preferred_element_type=f32) for m in range(lo, hi, most)], 0)
+def pieces(half, most=768):
+    return [(m, lo, min(lo + most, (m + 1) * half)) for m in BOTH for lo in range(m * half, (m + 1) * half, most)]
+
+
+def load_pieces(src, dst, half, sem):
+    return [(m, pltpu.make_async_copy(src.at[:, lo:hi], dst.at[:src.shape[0], lo:hi], sem.at[k])) for k, (m, lo, hi) in enumerate(pieces(half))]
+
+
+def down_products(k, j, act, rhs, loads):
+    for m in BOTH:
+        @pl.when(j == 0)
+        def _():
+            for which, c in loads:
+                if which == m:
+                    c.wait()
+        k.put_d(j, m, jnp.concatenate([lax.dot_general(act[:k.T, lo:hi], rhs, TN, preferred_element_type=f32) for which, lo, hi in pieces(k.half) if which == m], 0))
 
 
 def cols_of(j, w):
@@ -564,10 +578,8 @@
     def kernel(a_h, act_h, dgu_h, dy_h, h_h, w_h, og, ou, od, sq, dh_h,
                a_v, act_v, dg_v, dy_v, row_v, part_v, ld, ldg, ldy, ldr, ldo, ldw, *bufs):
         p = Place(n)
-        def load_act(m):
-            cols = pl.ds(m * k.half, k.half)
-            return pltpu.make_async_copy(act_h.at[:, cols], act_v.at[:T, cols], ld.at[m])
-        load_a = pltpu.make_async_copy(a_h, a_v, ld.at[2])
+        act_loads = load_pieces(act_h, act_v, k.half, ld)
+        load_a = pltpu.make_async_copy(a_h, a_v, ldw)
         def load_dy(j):
             return pltpu.make_async_copy(dy_h.at[:, cols_of(j, 2 * cd)], dy_v.at[lax.rem(j, 2)], ldy.at[lax.rem(j, 2)])
         def load_dg(j, e):
@@ -599,10 +611,12 @@
         def tile_of(v, m):
             return jnp.concatenate([v[pl.ds(pl.multiple_of(c * tile + m * part, part), part)] for c in range(k.nd)], 1)
         part = tile // 4
-        load_dy(0).start(); load_act(0).start(); load_act(1).start()
+        load_dy(0).start()
+        for _, c in act_loads:
+            c.start()
         barrier(p)
         k.streams(p, og, ou, od, sq, bufs)
-        load_dy(0).wait(); load_act(0).wait()
+        load_dy(0).wait()
         def make_d(j):
             @pl.when(j + 1 < k.nd)
             def _(): load_dy(j + 1).start()
@@ -611,11 +625,7 @@
             @pl.when(j == k.nd - 1)
             def _():
                 for e in BOTH: load_dg(0, e).start()
-            for m in BOTH:
-                if m == 1:
-                    @pl.when(j == 0)
-                    def _(): load_act(1).wait()
-                k.put_d(j, m, tall_product(act_v, m * k.half, (m + 1) * k.half, dy_v[lax.rem(j, 2)]))
+            down_products(k, j, act_v, dy_v[lax.rem(j, 2)], act_loads)
             k.sd.send(j)
             @pl.when(j + 1 < k.nd)
             def _(): load_dy(j + 1).wait()
@@ -625,8 +635,8 @@
                 for e in BOTH: load_dg(j + 1, e).start()
             @pl.when(j == 0)
             def _():
+                load_a.wait()
                 lax.fori_loop(0, n, lambda d, _: load_w(d), 0)
-                load_a.wait()
             @pl.when(j == k.ng - 1)
             def _():
                 for e in BOTH: load_row(0, e).start()
@@ -637,20 +647,24 @@
             k.put_g(j, lax.dot_general(a_v[...], dg_v[lax.rem(j, 2)], TN, preferred_element_type=f32))
             k.sg.send(j)
         def rows(i):
-            r, e = i // 2, lax.rem(i, 2)
+            r, e, s = i // 4, lax.rem(i // 2, 2), lax.rem(i, 2)
+            wide = Dm // 2
             @pl.when(i == 0)
             def _():
                 pltpu.make_async_copy(w_v, w_v, ldw).wait()
-            @pl.when((e == 0) & (r > 0))
+            @pl.when((e == 0) & (s == 0) & (r > 0))
             def _():
                 arrived(y_v, ldo)
                 load_y(r)
-            load_row(r, e).wait()
-            part_v[e] = lax.dot_general(row_v[e], act_v[pl.ds(pl.multiple_of(e * Dm, Dm), Dm)], NT, preferred_element_type=f32).astype(bf)
-            @pl.when(r + 1 < T // tile)
+            @pl.when(s == 0)
+            def _():
+                load_row(r, e).wait()
+            some = pl.ds(pl.multiple_of(s * wide, wide), wide)
+            part_v[e, :, some] = lax.dot_general(row_v[e], act_v[pl.ds(pl.multiple_of(e * Dm + s * wide, wide), wide)], NT, preferred_element_type=f32).astype(bf)
+            @pl.when((s == 1) & (r + 1 < T // tile))
             def _():
                 load_row(r + 1, e).start()
-            @pl.when(e == 1)
+            @pl.when((e == 1) & (s == 1))
             def _():
                 arrived(h_v, ldr.at[2])
                 arrived(y_v, ldr.at[3])
@@ -669,13 +683,13 @@
                 @pl.when(r + 1 < T // tile)
                 def _():
                     load_h(r + 1)
-        k.run(make_d, make_g, 2 * (T // tile), rows)
+        k.run(make_d, make_g, 4 * (T // tile), rows)
         arrived(y_v, ldo)
     V, A, D, VM = pl.BlockSpec(memory_space=pltpu.VMEM), pl.BlockSpec(memory_space=pl.ANY), pltpu.SemaphoreType.DMA, pltpu.VMEM
     return pl.pallas_call(
         kernel, name="backward_last", out_shape=[*k.outs(), jax.ShapeDtypeStruct((T, Dm), bf)], in_specs=[A] * 6, out_specs=[V] * 4 + [A],
         scratch_shapes=[VM((T, Dm), bf), VM((max(T, 2 * Dm), F), bf), VM((2, T, 2 * cg), bf), VM((2, T, 2 * cd), bf), VM((2, tile, F), bf), VM((2, tile, Dm), bf),
-                        D((3,)), D((2, 2)), D((2,)), D((4,)), D, D, *k.bufs()],
+                        D((4,)), D((2, 2)), D((2,)), D((4,)), D, D, *k.bufs()],
         compiler_params=pltpu.CompilerParams(collective_id=cid, has_side_effects=True, vmem_limit_bytes=67043328),
     )(a, act, dgu, dy, h, wgu)
 
@@ -683,23 +697,26 @@
 def backward_first(n, a, act, by_gate, by_up, dh, wd, sq_last, count, layer, lag=2, lagd=2, cg=256, cd=128, cid=3):
     k = Layer(n, a, act, lag, lagd, cg, cd)
     T, Dm, F, rows = k.T, k.Dm, k.F, k.T // 2
-    def kernel(a_h, act_h, g_h, u_h, dh_h, wd_h, sq_ref, og, ou, od, factor, a_v, act_v, gu_v, dg_v, dh_v, wd_v, ld, ldg, ldw, sq, part_v, got, send, recv, *bufs):
+    def kernel(a_h, act_h, g_h, u_h, dh_h, wd_h, sq_ref, og, ou, od, factor, a_v, act_v, gu_v, dg_v, dh_v, wd_v, ld, ldg, ldw, ldh, sq, part_v, got, send, recv, *bufs):
         p = Place(n)
-        def load_act(m):
-            cols = pl.ds(m * k.half, k.half)
-            return pltpu.make_async_copy(act_h.at[:, cols], act_v.at[:, cols], ld.at[m])
-        load_a = pltpu.make_async_copy(a_h, a_v, ld.at[2])
-        load_dh = pltpu.make_async_copy(dh_h, dh_v, ld.at[3])
+        act_loads = load_pieces(act_h, act_v, k.half, ld)
+        load_a = pltpu.make_async_copy(a_h, a_v, ldw)
+        def load_dh(j):
+            cols = cols_of(j, 2 * cd)
+            return pltpu.make_async_copy(dh_h.at[:, cols], dh_v.at[:, cols], ldh.at[j])
         def part(r):
             return pl.ds(pl.multiple_of(r * rows, rows), rows)
         def load_gu(j, r):
             return [pltpu.make_async_copy((g_h, u_h)[e].at[part(r), cols_of(j, cg)], gu_v.at[r, e], ldg.at[r, e]) for e in BOTH]
         def load_wd(j):
             return pltpu.make_async_copy(wd_h.at[layer, cols_of(j, cg), :], wd_v, ldw)
-        load_dh.start(); load_act(0).start(); load_act(1).start()
+        load_dh(0).start()
+        for _, c in act_loads:
+            c.start()
+        for j in range(1, k.nd):
+            load_dh(j).start()
         greet_all(n)
         k.streams(p, og, ou, od, sq, bufs)
-        load_dh.wait(); load_act(0).wait()
         def make_d(j):
             @pl.when(j == 0)
             def _(): load_a.start()
@@ -707,16 +724,12 @@
             def _():
                 for r in BOTH:
                     for c in load_gu(0, r): c.start()
+                load_a.wait()
                 load_wd(0).start()
-            for m in BOTH:
-                if m == 1:
-                    @pl.when(j == 0)
-                    def _(): load_act(1).wait()
-                k.put_d(j, m, tall_product(act_v, m * k.half, (m + 1) * k.half, dh_v[:, cols_of(j, 2 * cd)]))
+            load_dh(j).wait()
+            down_products(k, j, act_v, dh_v[:, cols_of(j, 2 * cd)], act_loads)
             k.sd.send(j)
         def make_g(j):
-            @pl.when(j == 0)
-            def _(): load_a.wait()
             load_wd(j).wait()
             def one(r, _):
                 for c in load_gu(j, r):
@@ -740,7 +753,7 @@
     return pl.pallas_call(
         kernel, name="backward_first", out_shape=k.outs(), in_specs=[A] * 6 + [V], out_specs=[V] * 4,
         scratch_shapes=[VM((T, Dm), bf), VM((T, F), bf), VM((2, 2, rows, cg), f32), VM((T, 2 * cg), bf), VM((T, Dm), bf), VM((cg, Dm), bf),
-                        D((4,)), D((2, 2)), D, VM((8, 128), f32), VM((8, 128), f32), VM((n, 8, 128), f32), D((n,)), D((n,)), *k.bufs()],
+                        D((4,)), D((2, 2)), D, D((k.nd,)), VM((8, 128), f32), VM((8, 128), f32), VM((n, 8, 128), f32), D((n,)), D((n,)), *k.bufs()],
         compiler_params=pltpu.CompilerParams(collective_id=cid, has_side_effects=True, vmem_limit_bytes=67043328),
     )(a, act, by_gate, by_up, dh, wd, sq_last)
 

time: 339 us -> 345 us (1.018)
  Pallas kernels: 337 us -> 344 us
    pallas_call x1, Pallas kernels: 92.4 us -> 98.3 us  [backward_last(): pl.pallas_call(kernel, name='backward_last', out_shape=[*k.outs(), jax.Sh...]
where the time goes in v4:
time: 345 us
  Pallas kernels  344 us (100%)
    pallas_call x1, Pallas kernels, forward(): pl.pallas_call(kernel, name='forward', out_shape=[S((L, side, side, 2, 2,...  140 us
    pallas_call x1, Pallas kernels, backward_first(): pl.pallas_call(kernel, name='backward_first', out_shape=k.outs(), in_spec...  99.4 us
    pallas_call x1, Pallas kernels, backward_last(): pl.pallas_call(kernel, name='backward_last', out_shape=[*k.outs(), jax.Sh...  98.3 us

profile of v4, /device:TPU:97, one launch (start us, length us, event | category | flops | bytes accessed | tf_op | source)
XLA Modules:
  0.0 345.2 jit_solution(11867943291647818436)
XLA Ops:
  0.6 140.4 %forward.1 = (bf16[2,4,4,2,2,32,2816]{6,5,4,3,2,1,0:T(8,128)(2,1)}, bf16[2,4,4,176,1024]{4,3,2,1,0:T(8,128)(2,1)}, f32[2048,2816]{1,0:T(8,128)}, f32[2048,2816]{...) custom-call(bf16[2048,1024]{1,0:T(8,128)(2,1)} %bitcast.6, ...), custom_call_target="tpu_custom_call" | custom-call | tf_op jit(solution)/shard_map/forward/pallas_call | solution.py:421
  141.1 98.3 %backward_last.1 = (bf16[32,2816]{1,0:T(8,128)(2,1)}, bf16[32,2816]{1,0:T(8,128)(2,1)}, bf16[88,1024]{1,0:T(8,128)(2,1)}, f32[8,128]{1,0:T(8,128)}, bf16[2048,1024]{1,0:T(8,128)(2,1)}) custom-call(bf16[2048,1024]{1,0:T(8,128)(2,1)} %get-tuple-element.32.a_h, bf16[2048,2816]{1,0:T(8,128)(2,1)} %get-tuple-element.33.act_h, ...), custom_call_target="tpu_custom_call" | custom-call | tf_op jit(solution)/shard_map/backward_last/pallas_call | solution.py:689
  239.4 99.4 %backward_first.1 = (bf16[32,2816]{1,0:T(8,128)(2,1)}, bf16[32,2816]{1,0:T(8,128)(2,1)}, bf16[88,1024]{1,0:T(8,128)(2,1)}, f32[8,128]{1,0:T(8,128)}) custom-call(bf16[2048,1024]{1,0:T(8,128)(2,1)} %get-tuple-element.28.a_h, bf16[2048,2816]{1,0:T(8,128)(2,1)} %get-tuple-element.29.act_h, f32[2048,2816]{1,0:T(8,128)} %get-tuple-element.30.g_h, ...), custom_call_target="tpu_custom_call" | custom-call | tf_op jit(solution)/shard_map/backward_first/pallas_call | solution.py:753
  338.8 6.2 %update.1 = (bf16[2,32,2816]{2,1,0:T(8,128)(2,1)}, bf16[2,32,2816]{2,1,0:T(8,128)(2,1)}, bf16[2,88,1024]{2,1,0:T(8,128)(2,1)}, f32[2,32,2816]{2,1,0:T(8,128)}, f...) custom-call(f32[8,128]{1,0:T(8,128)} %get-tuple-element.40.f_ref, ...), custom_call_target="tpu_custom_call" | custom-call | tf_op jit(solution)/shard_map/update/pallas_call | solution.py:484
